TPU v7x, 128 devices: a 2x2x16 block of a 8x8x16 slice. The times are simulated.
128 devices in a mesh: groups: 4 (over y, x), gx: 16 (over z), gy: 2 (over core).
Axes of the slice: x: 2, y: 2, z: 16, core: 2. Of those that a mesh axis runs over, the one named last changes fastest.
The devices are a block of a 8x8x16 slice.
Arguments:
- source: float32 [4, 3, 2, 64, 64, 256], P('groups', None, None, 'gx', 'gy'), parts along dimension 0, may hold values from -12 to 12
- permittivity: float32 [12, 64, 64, 256], P('groups', 'gx', 'gy'), parts along dimension 0, may hold values from 1 to 12
- frequency: float32 [1], replicated, may hold values from 0.25 to 0.6
Outputs:
- solution: float32 [4, 3, 2, 64, 64, 256], P('groups', None, None, 'gx', 'gy'), parts along dimension 0
- residual: float32 [4, 3, 2, 64, 64, 256], P('groups', None, None, 'gx', 'gy'), parts along dimension 0
There are 4 independent parts, one for each index of `groups`. A program takes and returns all parts, laid end to end along the dimension named above; an argument that names none is the same for every part. Nothing has to cross between parts.
All inputs are finite; a program needn't handle non-finite values.
Results may differ from a plain program's by a relative error of at most 0.0003.
Values sent between devices are 32-bit elements; how exact they have to be, the bound alone decides.
A program may use at most 64 MiB of HBM per device.

v0:
```python
import jax
import jax.numpy as jnp
from jax import lax
from jax.sharding import PartitionSpec as P

NZ = 256
PML = 8
ITERS = 3


pml_strength = 2.0


def with_halo(block, sides, width):
    for axis, dim in sides:
        count = lax.axis_size(axis)
        forward = [(i, i + 1) for i in range(count - 1)]
        backward = [(target, source) for source, target in forward]
        low = lax.ppermute(
            lax.slice_in_dim(block, block.shape[dim] - width, None, axis=dim), axis, forward
        )
        high = lax.ppermute(lax.slice_in_dim(block, 0, width, axis=dim), axis, backward)
        block = jnp.concatenate([low, block, high], axis=dim)
    return block


def sent_to_all(array, axis):
    copies = jnp.broadcast_to(array, (lax.axis_size(axis), *array.shape))
    return lax.all_to_all(copies, axis, split_axis=0, concat_axis=0, tiled=True)


def over_copies(array, axis):
    everything = sent_to_all(array, axis)
    return jnp.sum(everything, axis=0)


def in_one(arrays, axis):
    line, at, finished = (jnp.concatenate([a.reshape(-1) for a in arrays]), 0, [])
    running = over_copies(line, axis)
    for a in arrays:
        finished.append(running[at : at + a.size].reshape(a.shape))
        at += a.size
    return tuple(finished)


def stretch(points, length, frequency):
    inside = jnp.maximum(jnp.maximum(PML - points, points - (length - PML)), 0.0) / PML
    damping = pml_strength * inside**3 / frequency[:, None]
    factor = 1.0 / (1.0 + damping * damping)
    return jnp.stack([factor, -damping * factor], axis=1)


def orient(coefficient, dimension):
    target = [coefficient.shape[0], 2, 1, 1, 1]
    target[dimension] = coefficient.shape[2]
    return coefficient.reshape(target)


def times_coef(values, coefficient):
    real_part = values[:, 0] * coefficient[:, 0] - values[:, 1] * coefficient[:, 1]
    imag_part = values[:, 0] * coefficient[:, 1] + values[:, 1] * coefficient[:, 0]
    return jnp.stack([real_part, imag_part], axis=1)


def curl_forward(extended, front_x, front_y, front_z):
    centre = extended[:, :, :, :-1, :-1]

    def step_x(component):
        return extended[:, component, :, 1:, :-1] - centre[:, component]

    def step_y(component):
        return extended[:, component, :, :-1, 1:] - centre[:, component]

    def step_z(component):
        cells = centre[:, component]
        above = jnp.concatenate([cells[..., 1:], jnp.zeros_like(cells[..., :1])], axis=-1)
        return above - cells

    curl_x = times_coef(step_y(2), front_y) - times_coef(step_z(1), front_z)
    curl_y = times_coef(step_z(0), front_z) - times_coef(step_x(2), front_x)
    curl_z = times_coef(step_x(1), front_x) - times_coef(step_y(0), front_y)
    return jnp.stack([curl_x, curl_y, curl_z], axis=1)


def curl_backward(padded, back_x, back_y, back_z):
    centre = padded[:, :, :, 1:, 1:]

    def step_x(component):
        return centre[:, component] - padded[:, component, :, :-1, 1:]

    def step_y(component):
        return centre[:, component] - padded[:, component, :, 1:, :-1]

    def step_z(component):
        cells = centre[:, component]
        below = jnp.concatenate([jnp.zeros_like(cells[..., :1]), cells[..., :-1]], axis=-1)
        return cells - below

    out_x = times_coef(step_y(2), back_y) - times_coef(step_z(1), back_z)
    out_y = times_coef(step_z(0), back_z) - times_coef(step_x(2), back_x)
    out_z = times_coef(step_x(1), back_x) - times_coef(step_y(0), back_y)
    return jnp.stack([out_x, out_y, out_z], axis=1)


def scaled(values, number):
    real_scale = number[0].reshape(-1, 1, 1, 1, 1)
    imag_scale = number[1].reshape(-1, 1, 1, 1, 1)
    real_part = values[:, :, 0] * real_scale - values[:, :, 1] * imag_scale
    imag_part = values[:, :, 0] * imag_scale + values[:, :, 1] * real_scale
    return jnp.stack([real_part, imag_part], axis=2)


def product(left, right):
    real_part = jnp.sum(
        left[:, :, 0] * right[:, :, 0] + left[:, :, 1] * right[:, :, 1], axis=(1, 2, 3, 4)
    )
    imag_part = jnp.sum(
        left[:, :, 0] * right[:, :, 1] - left[:, :, 1] * right[:, :, 0], axis=(1, 2, 3, 4)
    )
    return jnp.stack([real_part, imag_part])


def complex_times(first, other):
    return jnp.stack(
        [first[0] * other[0] - first[1] * other[1], first[0] * other[1] + first[1] * other[0]]
    )


def complex_ratio(first, other):
    modulus = other[0] * other[0] + other[1] * other[1]
    return (
        jnp.stack(
            [first[0] * other[0] + first[1] * other[1], first[1] * other[0] - first[0] * other[1]]
        )
        / modulus
    )


def grid_points(start, first, count):
    return (start + jnp.arange(first, count, dtype=jnp.int32)).astype(jnp.float32)


def body(source, permittivity, frequency):
    cells_x = source.shape[3]
    cells_y = source.shape[4]
    total_x = cells_x * lax.axis_size("gx")
    total_y = cells_y * lax.axis_size("gy")
    index_x = lax.axis_index("gx")
    index_y = lax.axis_index("gy")
    margin = 1
    front_x = orient(
        stretch(grid_points(index_x * cells_x, -margin, cells_x) + 0.5, total_x, frequency), 2
    )
    front_y = orient(
        stretch(grid_points(index_y * cells_y, -margin, cells_y) + 0.5, total_y, frequency), 3
    )
    back_x = orient(stretch(grid_points(index_x * cells_x, 0, cells_x), total_x, frequency), 2)
    back_y = orient(stretch(grid_points(index_y * cells_y, 0, cells_y), total_y, frequency), 3)
    z_points = grid_points(0, 0, NZ)
    front_z = orient(stretch(z_points + 0.5, NZ, frequency), 4)
    back_z = orient(stretch(z_points, NZ, frequency), 4)
    material = (frequency * frequency).reshape(-1, 1, 1, 1, 1, 1) * permittivity[None, :, None]

    def operate(values):
        extended = with_halo(values, (("gx", 3), ("gy", 4)), 1)
        keep_x = jnp.where((jnp.arange(cells_x + 1) > 0) | (index_x > 0), 1.0, 0.0).astype(
            jnp.float32
        )
        keep_y = jnp.where((jnp.arange(cells_y + 1) > 0) | (index_y > 0), 1.0, 0.0).astype(
            jnp.float32
        )
        rotated = curl_forward(extended, front_x, front_y, front_z)
        padded = rotated * keep_x.reshape(1, 1, 1, -1, 1, 1) * keep_y.reshape(1, 1, 1, 1, -1, 1)
        applied = curl_backward(padded, back_x, back_y, back_z)
        return applied - material * values

    solution = jnp.zeros_like(source)
    residual = source
    direction = source
    shadow_dot = over_copies(product(source, residual), ("gx", "gy"))
    for iteration in range(ITERS):
        applied = operate(direction)
        step_size = complex_ratio(shadow_dot, over_copies(product(source, applied), ("gx", "gy")))
        middle = residual - scaled(applied, step_size)
        second = operate(middle)
        sums_triple = in_one(
            (product(second, middle), product(second, second), product(source, second)),
            ("gx", "gy"),
        )
        weight = complex_ratio(sums_triple[0], sums_triple[1])
        solution = solution + scaled(direction, step_size) + scaled(middle, weight)
        residual = middle - scaled(second, weight)
        if iteration + 1 < ITERS:
            shadow_next = -complex_times(weight, sums_triple[2])
            momentum = complex_times(
                complex_ratio(shadow_next, shadow_dot), complex_ratio(step_size, weight)
            )
            direction = residual + scaled(direction - scaled(applied, weight), momentum)
            shadow_dot = shadow_next
    return (solution, residual)


def solution(mesh):
    placed = (P("groups", None, None, "gx", "gy", None), P("groups", "gx", "gy", None), P())
    return jax.shard_map(
        body,
        mesh=mesh,
        in_specs=placed,
        out_specs=(
            P("groups", None, None, "gx", "gy", None),
            P("groups", None, None, "gx", "gy", None),
        ),
        check_vma=False,
    )
```

profile of v0, /device:TPU:69, one launch (start us, length us, event | category | flops | bytes accessed | tf_op | source)
XLA Modules:
  0.0 425.0 jit_solution(13874893840532838654)
XLA Ops:
  3.1 5.2 %collective-permute-start = (f32[1,3,2,1,32,256]{5,4,3,2,1,0:T(8,128)S(1)}, f32[1,3,2,1,32,256]{5,4,3,2,1,0:T(8,128)S(1)}, u32[]{:S(2)}, u32[]{:S(2)}) collective-permute-start(f32[1,3,2,1,32,256]{5,4,3,2,1,0:T(8,128)S(1)} %get-tuple-element.185), channel_id=1, source_target_pairs={{0,2},{2,4},{4,6},{6,8},{8,10},{10,12},{12,14},{14,16},{16,18},{18... | collective-permute-start | bytes 589832 | tf_op jit(solution)/shard_map/ppermute | solution.py:19
  11.1 11.8 %collective-permute-start.2 = (f32[1,3,2,6,1,256]{5,4,3,2,1,0:T(1,128)S(1)}, f32[1,3,2,6,1,256]{5,4,3,2,1,0:T(1,128)S(1)}, u32[]{:S(2)}, u32[]{:S(2)}) collective-permute-start(f32[1,3,2,6,1,256]{5,4,3,2,1,0:T(1,128)S(1)} %get-tuple-element.134), channel_id=1, source_target_pairs={{1,0},{3,2},{5,4},{7,6},{9,8},{11,10},{13,12},{15,14},{17,16},{19,... | collective-permute-start | bytes 110600 | tf_op jit(solution)/shard_map/ppermute | solution.py:22
  31.6 11.5 %all-to-all-start = ((f32[32,2,1]{1,2,0:T(1,128)}), f32[32,2,1]{1,2,0:T(1,128)S(1)}, u32[]{:S(2)}, u32[]{:S(2)}) async-start(f32[32,2,1]{1,2,0:T(1,128)} %broadcast_in_dim.76), calls=%async_computation | async-start | bytes 32768 | tf_op jit(solution)/shard_map/all_to_all | solution.py:29
  44.4 10.2 %all-to-all-done = f32[32,2,1]{1,2,0:T(1,128)S(1)} async-done(((f32[32,2,1]{1,2,0:T(1,128)}), f32[32,2,1]{1,2,0:T(1,128)S(1)}, u32[]{:S(2)}, u32[]{:S(2)}) %all-to-all-start) | async-done | bytes 288 | tf_op jit(solution)/shard_map/all_to_all | solution.py:29
  55.2 4.7 %all-to-all-start.1 = ((f32[32,2,1]{1,2,0:T(1,128)}), f32[32,2,1]{1,2,0:T(1,128)S(1)}, u32[]{:S(2)}, u32[]{:S(2)}) async-start(f32[32,2,1]{1,2,0:T(1,128)} %broadcast_in_dim.79), calls=%async_computation.1 | async-start | bytes 32768 | tf_op jit(solution)/shard_map/all_to_all | solution.py:29
  60.6 11.1 %all-to-all-done.1 = f32[32,2,1]{1,2,0:T(1,128)S(1)} async-done(((f32[32,2,1]{1,2,0:T(1,128)}), f32[32,2,1]{1,2,0:T(1,128)S(1)}, u32[]{:S(2)}, u32[]{:S(2)}) %all-to-all-start.1) | async-done | bytes 288 | tf_op jit(solution)/shard_map/all_to_all | solution.py:29
  87.5 3.9 collective-permute-done.5
  92.7 4.1 collective-permute-start.6
  108.7 5.9 %all-to-all-start.2 = ((f32[32,1,6]{2,1,0:T(1,128)}), f32[32,1,6]{2,1,0:T(1,128)S(1)}, u32[]{:S(2)}, u32[]{:S(2)}) async-start(f32[32,1,6]{2,1,0:T(1,128)} %broadcast_in_dim.80), calls=%async_computation.2 | async-start | bytes 32768 | tf_op jit(solution)/shard_map/all_to_all | solution.py:29
  117.2 9.0 %all-to-all-done.2 = f32[32,1,6]{2,1,0:T(1,128)S(1)} async-done(((f32[32,1,6]{2,1,0:T(1,128)}), f32[32,1,6]{2,1,0:T(1,128)S(1)}, u32[]{:S(2)}, u32[]{:S(2)}) %all-to-all-start.2) | async-done | bytes 800 | tf_op jit(solution)/shard_map/all_to_all | solution.py:29
  170.5 3.9 collective-permute-done.9
  175.7 4.2 collective-permute-start.10
  188.5 17.5 %all_to_all.38 = f32[32,2,1]{1,2,0:T(1,128)S(1)} all-to-all(f32[32,2,1]{1,2,0:T(1,128)S(1)} %broadcast_in_dim.81), channel_id=1, replica_groups=mesh['groups'=4,'gx'=16,'gy'=2] {'gx','gy'}, dimensions={0} | all-to-all | bytes 512 | tf_op jit(solution)/shard_map/all_to_all | solution.py:29
  214.5 2.4 multiply_subtract_fusion.8
  222.8 3.9 collective-permute-done.13
  228.1 4.0 collective-permute-start.14
  244.2 6.1 %all-to-all-start.4 = ((f32[32,1,6]{2,1,0:T(1,128)}), f32[32,1,6]{2,1,0:T(1,128)S(1)}, u32[]{:S(2)}, u32[]{:S(2)}) async-start(f32[32,1,6]{2,1,0:T(1,128)} %broadcast_in_dim.82), calls=%async_computation.4 | async-start | bytes 32768 | tf_op jit(solution)/shard_map/all_to_all | solution.py:29
  252.8 9.1 %all-to-all-done.4 = f32[32,1,6]{2,1,0:T(1,128)S(1)} async-done(((f32[32,1,6]{2,1,0:T(1,128)}), f32[32,1,6]{2,1,0:T(1,128)S(1)}, u32[]{:S(2)}, u32[]{:S(2)}) %all-to-all-start.4) | async-done | bytes 800 | tf_op jit(solution)/shard_map/all_to_all | solution.py:29
  297.0 2.6 multiply_subtract_fusion.5
  308.6 3.9 collective-permute-done.17
  313.8 4.2 collective-permute-start.18
  328.2 6.1 %all-to-all-start.5 = ((f32[32,2,1]{1,2,0:T(1,128)}), f32[32,2,1]{1,2,0:T(1,128)S(1)}, u32[]{:S(2)}, u32[]{:S(2)}) async-start(f32[32,2,1]{1,2,0:T(1,128)} %broadcast_in_dim.83), calls=%async_computation.5 | async-start | bytes 32768 | tf_op jit(solution)/shard_map/all_to_all | solution.py:29
  336.6 9.3 %all-to-all-done.5 = f32[32,2,1]{1,2,0:T(1,128)S(1)} async-done(((f32[32,2,1]{1,2,0:T(1,128)}), f32[32,2,1]{1,2,0:T(1,128)S(1)}, u32[]{:S(2)}, u32[]{:S(2)}) %all-to-all-start.5) | async-done | bytes 288 | tf_op jit(solution)/shard_map/all_to_all | solution.py:29
  354.9 2.4 multiply_subtract_fusion.2
  363.9 3.6 collective-permute-done.21
  368.9 2.4 multiply_subtract_fusion.7
  371.2 4.0 collective-permute-start.22
  381.9 3.2 add_reduce_fusion.2
  389.5 6.1 %all-to-all-start.6 = ((f32[32,1,6]{2,1,0:T(1,128)}), f32[32,1,6]{2,1,0:T(1,128)S(1)}, u32[]{:S(2)}, u32[]{:S(2)}) async-start(f32[32,1,6]{2,1,0:T(1,128)} %broadcast_in_dim.84), calls=%async_computation.6 | async-start | bytes 32768 | tf_op jit(solution)/shard_map/all_to_all | solution.py:29
  395.7 3.4 multiply_subtract_fusion.3
  399.1 8.2 %all-to-all-done.6 = f32[32,1,6]{2,1,0:T(1,128)S(1)} async-done(((f32[32,1,6]{2,1,0:T(1,128)}), f32[32,1,6]{2,1,0:T(1,128)S(1)}, u32[]{:S(2)}, u32[]{:S(2)}) %all-to-all-start.6) | async-done | bytes 800 | tf_op jit(solution)/shard_map/all_to_all | solution.py:29
  417.1 2.7 multiply_subtract_fusion
  (524 shorter events, 134.1 us)
Async XLA Ops:
  1.8 9.2 %collective-permute-start.1 = (f32[1,3,2,1,32,256]{5,4,3,2,1,0:T(8,128)S(1)}, f32[1,3,2,1,32,256]{5,4,3,2,1,0:T(8,128)S(1)}, u32[]{:S(2)}, u32[]{:S(2)}) collective-permute-start(f32[1,3,2,1,32,256]{5,4,3,2,1,0:T(8,128)S(1)} %get-tuple-element.184), channel_id=1, source_target_pairs={{2,0},{4,2},{6,4},{8,6},{10,8},{12,10},{14,12},{16,14},{18,16},{20... | collective-permute-start | bytes 589832 | tf_op jit(solution)/shard_map/ppermute | solution.py:22
  3.1 7.8 %collective-permute-start = (f32[1,3,2,1,32,256]{5,4,3,2,1,0:T(8,128)S(1)}, f32[1,3,2,1,32,256]{5,4,3,2,1,0:T(8,128)S(1)}, u32[]{:S(2)}, u32[]{:S(2)}) collective-permute-start(f32[1,3,2,1,32,256]{5,4,3,2,1,0:T(8,128)S(1)} %get-tuple-element.185), channel_id=1, source_target_pairs={{0,2},{2,4},{4,6},{6,8},{8,10},{10,12},{12,14},{14,16},{16,18},{18... | collective-permute-start | bytes 589832 | tf_op jit(solution)/shard_map/ppermute | solution.py:19
  9.3 91.4 %copy-start.53 = (f32[1,1,1,1,256]{4,1,3,2,0:T(1,128)}, f32[1,1,1,1,256]{4,1,3,2,0:T(1,128)S(1)}, u32[]{:S(2)}) copy-start(f32[1,1,1,1,256]{4,1,3,2,0:T(1,128)S(1)} %get-tuple-element.352) | copy-start | bytes 3076
  10.4 174.5 %copy-start.10 = (f32[3,4,32,256]{3,2,1,0:T(8,128)}, f32[3,4,32,256]{3,2,1,0:T(8,128)S(1)}, u32[]{:S(2)}) copy-start(f32[3,4,32,256]{3,2,1,0:T(8,128)S(1)} %broadcast_multiply_fusion) | copy-start | bytes 1179652
  11.1 13.1 %collective-permute-start.2 = (f32[1,3,2,6,1,256]{5,4,3,2,1,0:T(1,128)S(1)}, f32[1,3,2,6,1,256]{5,4,3,2,1,0:T(1,128)S(1)}, u32[]{:S(2)}, u32[]{:S(2)}) collective-permute-start(f32[1,3,2,6,1,256]{5,4,3,2,1,0:T(1,128)S(1)} %get-tuple-element.134), channel_id=1, source_target_pairs={{1,0},{3,2},{5,4},{7,6},{9,8},{11,10},{13,12},{15,14},{17,16},{19,... | collective-permute-start | bytes 110600 | tf_op jit(solution)/shard_map/ppermute | solution.py:22
  22.9 3.1 collective-permute-start.3
  31.6 23.0 %all-to-all-start = ((f32[32,2,1]{1,2,0:T(1,128)}), f32[32,2,1]{1,2,0:T(1,128)S(1)}, u32[]{:S(2)}, u32[]{:S(2)}) async-start(f32[32,2,1]{1,2,0:T(1,128)} %broadcast_in_dim.76), calls=%async_computation | async-start | bytes 32768 | tf_op jit(solution)/shard_map/all_to_all | solution.py:29
  55.2 16.5 %all-to-all-start.1 = ((f32[32,2,1]{1,2,0:T(1,128)}), f32[32,2,1]{1,2,0:T(1,128)S(1)}, u32[]{:S(2)}, u32[]{:S(2)}) async-start(f32[32,2,1]{1,2,0:T(1,128)} %broadcast_in_dim.79), calls=%async_computation.1 | async-start | bytes 32768 | tf_op jit(solution)/shard_map/all_to_all | solution.py:29
  82.1 5.4 %collective-permute-start.4 = (f32[1,3,2,1,32,256]{5,4,3,2,1,0:T(8,128)S(1)}, f32[1,3,2,1,32,256]{5,4,3,2,1,0:T(8,128)S(1)}, u32[]{:S(2)}, u32[]{:S(2)}) collective-permute-start(f32[1,3,2,1,32,256]{5,4,3,2,1,0:T(8,128)S(1)} %get-tuple-element.180), channel_id=1, source_target_pairs={{0,2},{2,4},{4,6},{6,8},{8,10},{10,12},{12,14},{14,16},{16,18},{18... | collective-permute-start | bytes 589832 | tf_op jit(solution)/shard_map/ppermute | solution.py:19
  84.2 7.1 %collective-permute-start.5 = (f32[1,3,2,1,32,256]{5,4,3,2,1,0:T(8,128)S(1)}, f32[1,3,2,1,32,256]{5,4,3,2,1,0:T(8,128)S(1)}, u32[]{:S(2)}, u32[]{:S(2)}) collective-permute-start(f32[1,3,2,1,32,256]{5,4,3,2,1,0:T(8,128)S(1)} %get-tuple-element.181), channel_id=1, source_target_pairs={{2,0},{4,2},{6,4},{8,6},{10,8},{12,10},{14,12},{16,14},{18,16},{20... | collective-permute-start | bytes 589832 | tf_op jit(solution)/shard_map/ppermute | solution.py:22
  91.4 5.4 %collective-permute-start.7 = (f32[1,3,2,6,1,256]{5,4,3,2,1,0:T(1,128)S(1)}, f32[1,3,2,6,1,256]{5,4,3,2,1,0:T(1,128)S(1)}, u32[]{:S(2)}, u32[]{:S(2)}) collective-permute-start(f32[1,3,2,6,1,256]{5,4,3,2,1,0:T(1,128)S(1)} %get-tuple-element.133), channel_id=1, source_target_pairs={{0,1},{2,3},{4,5},{6,7},{8,9},{10,11},{12,13},{14,15},{16,17},{18,... | collective-permute-start | bytes 110600 | tf_op jit(solution)/shard_map/ppermute | solution.py:19
  92.7 4.9 %collective-permute-start.6 = (f32[1,3,2,6,1,256]{5,4,3,2,1,0:T(1,128)S(1)}, f32[1,3,2,6,1,256]{5,4,3,2,1,0:T(1,128)S(1)}, u32[]{:S(2)}, u32[]{:S(2)}) collective-permute-start(f32[1,3,2,6,1,256]{5,4,3,2,1,0:T(1,128)S(1)} %get-tuple-element.132), channel_id=1, source_target_pairs={{1,0},{3,2},{5,4},{7,6},{9,8},{11,10},{13,12},{15,14},{17,16},{19,... | collective-permute-start | bytes 110600 | tf_op jit(solution)/shard_map/ppermute | solution.py:22
  108.7 17.5 %all-to-all-start.2 = ((f32[32,1,6]{2,1,0:T(1,128)}), f32[32,1,6]{2,1,0:T(1,128)S(1)}, u32[]{:S(2)}, u32[]{:S(2)}) async-start(f32[32,1,6]{2,1,0:T(1,128)} %broadcast_in_dim.80), calls=%async_computation.2 | async-start | bytes 32768 | tf_op jit(solution)/shard_map/all_to_all | solution.py:29
  165.0 5.5 %collective-permute-start.8 = (f32[1,3,2,1,32,256]{5,4,3,2,1,0:T(8,128)S(1)}, f32[1,3,2,1,32,256]{5,4,3,2,1,0:T(8,128)S(1)}, u32[]{:S(2)}, u32[]{:S(2)}) collective-permute-start(f32[1,3,2,1,32,256]{5,4,3,2,1,0:T(8,128)S(1)} %get-tuple-element.168), channel_id=1, source_target_pairs={{0,2},{2,4},{4,6},{6,8},{8,10},{10,12},{12,14},{14,16},{16,18},{18... | collective-permute-start | bytes 589832 | tf_op jit(solution)/shard_map/ppermute | solution.py:19
  167.2 7.2 %collective-permute-start.9 = (f32[1,3,2,1,32,256]{5,4,3,2,1,0:T(8,128)S(1)}, f32[1,3,2,1,32,256]{5,4,3,2,1,0:T(8,128)S(1)}, u32[]{:S(2)}, u32[]{:S(2)}) collective-permute-start(f32[1,3,2,1,32,256]{5,4,3,2,1,0:T(8,128)S(1)} %get-tuple-element.169), channel_id=1, source_target_pairs={{2,0},{4,2},{6,4},{8,6},{10,8},{12,10},{14,12},{16,14},{18,16},{20... | collective-permute-start | bytes 589832 | tf_op jit(solution)/shard_map/ppermute | solution.py:22
  174.4 5.5 %collective-permute-start.11 = (f32[1,3,2,6,1,256]{5,4,3,2,1,0:T(1,128)S(1)}, f32[1,3,2,6,1,256]{5,4,3,2,1,0:T(1,128)S(1)}, u32[]{:S(2)}, u32[]{:S(2)}) collective-permute-start(f32[1,3,2,6,1,256]{5,4,3,2,1,0:T(1,128)S(1)} %get-tuple-element.131), channel_id=1, source_target_pairs={{0,1},{2,3},{4,5},{6,7},{8,9},{10,11},{12,13},{14,15},{16,17},{18,... | collective-permute-start | bytes 110600 | tf_op jit(solution)/shard_map/ppermute | solution.py:19
  175.7 4.9 %collective-permute-start.10 = (f32[1,3,2,6,1,256]{5,4,3,2,1,0:T(1,128)S(1)}, f32[1,3,2,6,1,256]{5,4,3,2,1,0:T(1,128)S(1)}, u32[]{:S(2)}, u32[]{:S(2)}) collective-permute-start(f32[1,3,2,6,1,256]{5,4,3,2,1,0:T(1,128)S(1)} %get-tuple-element.130), channel_id=1, source_target_pairs={{1,0},{3,2},{5,4},{7,6},{9,8},{11,10},{13,12},{15,14},{17,16},{19,... | collective-permute-start | bytes 110600 | tf_op jit(solution)/shard_map/ppermute | solution.py:22
  217.3 5.5 %collective-permute-start.12 = (f32[1,3,2,1,32,256]{5,4,3,2,1,0:T(8,128)S(1)}, f32[1,3,2,1,32,256]{5,4,3,2,1,0:T(8,128)S(1)}, u32[]{:S(2)}, u32[]{:S(2)}) collective-permute-start(f32[1,3,2,1,32,256]{5,4,3,2,1,0:T(8,128)S(1)} %get-tuple-element.162), channel_id=1, source_target_pairs={{0,2},{2,4},{4,6},{6,8},{8,10},{10,12},{12,14},{14,16},{16,18},{18... | collective-permute-start | bytes 589832 | tf_op jit(solution)/shard_map/ppermute | solution.py:19
  219.5 7.2 %collective-permute-start.13 = (f32[1,3,2,1,32,256]{5,4,3,2,1,0:T(8,128)S(1)}, f32[1,3,2,1,32,256]{5,4,3,2,1,0:T(8,128)S(1)}, u32[]{:S(2)}, u32[]{:S(2)}) collective-permute-start(f32[1,3,2,1,32,256]{5,4,3,2,1,0:T(8,128)S(1)} %get-tuple-element.163), channel_id=1, source_target_pairs={{2,0},{4,2},{6,4},{8,6},{10,8},{12,10},{14,12},{16,14},{18,16},{20... | collective-permute-start | bytes 589832 | tf_op jit(solution)/shard_map/ppermute | solution.py:22
  226.7 5.4 %collective-permute-start.15 = (f32[1,3,2,6,1,256]{5,4,3,2,1,0:T(1,128)S(1)}, f32[1,3,2,6,1,256]{5,4,3,2,1,0:T(1,128)S(1)}, u32[]{:S(2)}, u32[]{:S(2)}) collective-permute-start(f32[1,3,2,6,1,256]{5,4,3,2,1,0:T(1,128)S(1)} %get-tuple-element.129), channel_id=1, source_target_pairs={{0,1},{2,3},{4,5},{6,7},{8,9},{10,11},{12,13},{14,15},{16,17},{18,... | collective-permute-start | bytes 110600 | tf_op jit(solution)/shard_map/ppermute | solution.py:19
  228.1 4.9 %collective-permute-start.14 = (f32[1,3,2,6,1,256]{5,4,3,2,1,0:T(1,128)S(1)}, f32[1,3,2,6,1,256]{5,4,3,2,1,0:T(1,128)S(1)}, u32[]{:S(2)}, u32[]{:S(2)}) collective-permute-start(f32[1,3,2,6,1,256]{5,4,3,2,1,0:T(1,128)S(1)} %get-tuple-element.128), channel_id=1, source_target_pairs={{1,0},{3,2},{5,4},{7,6},{9,8},{11,10},{13,12},{15,14},{17,16},{19,... | collective-permute-start | bytes 110600 | tf_op jit(solution)/shard_map/ppermute | solution.py:22
  244.2 17.7 %all-to-all-start.4 = ((f32[32,1,6]{2,1,0:T(1,128)}), f32[32,1,6]{2,1,0:T(1,128)S(1)}, u32[]{:S(2)}, u32[]{:S(2)}) async-start(f32[32,1,6]{2,1,0:T(1,128)} %broadcast_in_dim.82), calls=%async_computation.4 | async-start | bytes 32768 | tf_op jit(solution)/shard_map/all_to_all | solution.py:29
  303.1 5.5 %collective-permute-start.16 = (f32[1,3,2,1,32,256]{5,4,3,2,1,0:T(8,128)S(1)}, f32[1,3,2,1,32,256]{5,4,3,2,1,0:T(8,128)S(1)}, u32[]{:S(2)}, u32[]{:S(2)}) collective-permute-start(f32[1,3,2,1,32,256]{5,4,3,2,1,0:T(8,128)S(1)} %get-tuple-element.150), channel_id=1, source_target_pairs={{0,2},{2,4},{4,6},{6,8},{8,10},{10,12},{12,14},{14,16},{16,18},{18... | collective-permute-start | bytes 589832 | tf_op jit(solution)/shard_map/ppermute | solution.py:19
  305.2 7.2 %collective-permute-start.17 = (f32[1,3,2,1,32,256]{5,4,3,2,1,0:T(8,128)S(1)}, f32[1,3,2,1,32,256]{5,4,3,2,1,0:T(8,128)S(1)}, u32[]{:S(2)}, u32[]{:S(2)}) collective-permute-start(f32[1,3,2,1,32,256]{5,4,3,2,1,0:T(8,128)S(1)} %get-tuple-element.151), channel_id=1, source_target_pairs={{2,0},{4,2},{6,4},{8,6},{10,8},{12,10},{14,12},{16,14},{18,16},{20... | collective-permute-start | bytes 589832 | tf_op jit(solution)/shard_map/ppermute | solution.py:22
  312.5 5.5 %collective-permute-start.19 = (f32[1,3,2,6,1,256]{5,4,3,2,1,0:T(1,128)S(1)}, f32[1,3,2,6,1,256]{5,4,3,2,1,0:T(1,128)S(1)}, u32[]{:S(2)}, u32[]{:S(2)}) collective-permute-start(f32[1,3,2,6,1,256]{5,4,3,2,1,0:T(1,128)S(1)} %get-tuple-element.127), channel_id=1, source_target_pairs={{0,1},{2,3},{4,5},{6,7},{8,9},{10,11},{12,13},{14,15},{16,17},{18,... | collective-permute-start | bytes 110600 | tf_op jit(solution)/shard_map/ppermute | solution.py:19
  313.8 4.8 %collective-permute-start.18 = (f32[1,3,2,6,1,256]{5,4,3,2,1,0:T(1,128)S(1)}, f32[1,3,2,6,1,256]{5,4,3,2,1,0:T(1,128)S(1)}, u32[]{:S(2)}, u32[]{:S(2)}) collective-permute-start(f32[1,3,2,6,1,256]{5,4,3,2,1,0:T(1,128)S(1)} %get-tuple-element.126), channel_id=1, source_target_pairs={{1,0},{3,2},{5,4},{7,6},{9,8},{11,10},{13,12},{15,14},{17,16},{19,... | collective-permute-start | bytes 110600 | tf_op jit(solution)/shard_map/ppermute | solution.py:22
  328.2 17.7 %all-to-all-start.5 = ((f32[32,2,1]{1,2,0:T(1,128)}), f32[32,2,1]{1,2,0:T(1,128)S(1)}, u32[]{:S(2)}, u32[]{:S(2)}) async-start(f32[32,2,1]{1,2,0:T(1,128)} %broadcast_in_dim.83), calls=%async_computation.5 | async-start | bytes 32768 | tf_op jit(solution)/shard_map/all_to_all | solution.py:29
  357.9 6.0 %collective-permute-start.20 = (f32[1,3,2,1,32,256]{5,4,3,2,1,0:T(8,128)S(1)}, f32[1,3,2,1,32,256]{5,4,3,2,1,0:T(8,128)S(1)}, u32[]{:S(2)}, u32[]{:S(2)}) collective-permute-start(f32[1,3,2,1,32,256]{5,4,3,2,1,0:T(8,128)S(1)} %get-tuple-element.144), channel_id=1, source_target_pairs={{0,2},{2,4},{4,6},{6,8},{8,10},{10,12},{12,14},{14,16},{16,18},{18... | collective-permute-start | bytes 589832 | tf_op jit(solution)/shard_map/ppermute | solution.py:19
  360.2 7.3 %collective-permute-start.21 = (f32[1,3,2,1,32,256]{5,4,3,2,1,0:T(8,128)S(1)}, f32[1,3,2,1,32,256]{5,4,3,2,1,0:T(8,128)S(1)}, u32[]{:S(2)}, u32[]{:S(2)}) collective-permute-start(f32[1,3,2,1,32,256]{5,4,3,2,1,0:T(8,128)S(1)} %get-tuple-element.145), channel_id=1, source_target_pairs={{2,0},{4,2},{6,4},{8,6},{10,8},{12,10},{14,12},{16,14},{18,16},{20... | collective-permute-start | bytes 589832 | tf_op jit(solution)/shard_map/ppermute | solution.py:22
  367.6 7.7 %collective-permute-start.23 = (f32[1,3,2,6,1,256]{5,4,3,2,1,0:T(1,128)S(1)}, f32[1,3,2,6,1,256]{5,4,3,2,1,0:T(1,128)S(1)}, u32[]{:S(2)}, u32[]{:S(2)}) collective-permute-start(f32[1,3,2,6,1,256]{5,4,3,2,1,0:T(1,128)S(1)} %get-tuple-element.125), channel_id=1, source_target_pairs={{0,1},{2,3},{4,5},{6,7},{8,9},{10,11},{12,13},{14,15},{16,17},{18,... | collective-permute-start | bytes 110600 | tf_op jit(solution)/shard_map/ppermute | solution.py:19
  371.2 4.8 %collective-permute-start.22 = (f32[1,3,2,6,1,256]{5,4,3,2,1,0:T(1,128)S(1)}, f32[1,3,2,6,1,256]{5,4,3,2,1,0:T(1,128)S(1)}, u32[]{:S(2)}, u32[]{:S(2)}) collective-permute-start(f32[1,3,2,6,1,256]{5,4,3,2,1,0:T(1,128)S(1)} %get-tuple-element.124), channel_id=1, source_target_pairs={{1,0},{3,2},{5,4},{7,6},{9,8},{11,10},{13,12},{15,14},{17,16},{19,... | collective-permute-start | bytes 110600 | tf_op jit(solution)/shard_map/ppermute | solution.py:22
  389.5 17.7 %all-to-all-start.6 = ((f32[32,1,6]{2,1,0:T(1,128)}), f32[32,1,6]{2,1,0:T(1,128)S(1)}, u32[]{:S(2)}, u32[]{:S(2)}) async-start(f32[32,1,6]{2,1,0:T(1,128)} %broadcast_in_dim.84), calls=%async_computation.6 | async-start | bytes 32768 | tf_op jit(solution)/shard_map/all_to_all | solution.py:29
  (119 other events, 868.1 us)
where the time goes:
time: 428 us; the launch traced here: 425 us
  starting transfers between devices  105 us (25%)
  between operations  100 us (23%)
  waiting for transfers between devices  89 us (21%)
  other arithmetic  76.9 us (18%)
  local copies, waits for them, and re-layouts  36.4 us (9%)
  blocking collectives  17.5 us (4%)
    all_to_all x6, waiting for transfers between devices, sent_to_all(): return lax.all_to_all(copies, axis, split_axis=0, concat_axis=0, tiled=True)  56.8 us
    all_to_all x6, starting transfers between devices, sent_to_all(): return lax.all_to_all(copies, axis, split_axis=0, concat_axis=0, tiled=True)  40.5 us
    ppermute x12, starting transfers between devices, with_halo(): lax.ppermute(lax.slice_in_dim(block, 0, width, axis=dim), axis, backward)  40.2 us
    sub x15, other arithmetic, scaled(): real_part = values[:, :, 0] * real_scale - values[:, :, 1] * imag_scale  27.6 us
    ppermute x12, starting transfers between devices, with_halo(): lax.ppermute(lax.slice_in_dim(block, block.shape[dim] - width, None, axis...  24.1 us
    ppermute x12, waiting for transfers between devices, with_halo(): lax.ppermute(lax.slice_in_dim(block, 0, width, axis=dim), axis, backward)  22 us
    all_to_all x1, blocking collectives, sent_to_all(): return lax.all_to_all(copies, axis, split_axis=0, concat_axis=0, tiled=True)  17.5 us
    unnamed x244, local copies, waits for them, and re-layouts  15.5 us
  transfers between devices with their start and end apart: 30, of which 22 were waited for; matrix products, arithmetic and copies ran while one was open for 3% of the time, Pallas kernels for 0%

commit v1 on v0

v1 whole, which is shorter than its diff:
```python
import functools

import jax
import jax.numpy as jnp
from jax import lax
from jax.experimental import pallas as pl
from jax.experimental.pallas import tpu as pltpu
from jax.sharding import PartitionSpec as P

PML = 8
ITERS = 3
STRENGTH = 2.0
STEPS = 2 * ITERS
CX, CZ, CY = 0, 1, 2
ORDER = (0, 2, 1)
LANES = 128
TILE = 8
VALUES = 19

f32 = jnp.float32


def iota(shape, axis):
    return lax.broadcasted_iota(jnp.int32, shape, axis)


def stretch(points, length, freq):
    inside = jnp.maximum(jnp.maximum(PML - points, points - (length - PML)), 0.0) / PML
    damping = STRENGTH * (inside * inside * inside) / freq
    factor = 1.0 / (1.0 + damping * damping)
    return factor, -damping * factor


def cmul(a, b):
    return a[0] * b[0] - a[1] * b[1], a[0] * b[1] + a[1] * b[0]


def cadd(a, b):
    return a[0] + b[0], a[1] + b[1]


def csub(a, b):
    return a[0] - b[0], a[1] - b[1]


def cneg(a):
    return -a[0], -a[1]


def conj(a):
    return a[0], -a[1]


def cscale(a, s):
    return a[0] * s, a[1] * s


def cdiv(a, b):
    modulus = b[0] * b[0] + b[1] * b[1]
    return (a[0] * b[0] + a[1] * b[1]) / modulus, (a[1] * b[0] - a[0] * b[1]) / modulus


def z_up(pair):
    last = iota(pair[0].shape, 1) == LANES - 1
    low, high = pltpu.roll(pair[0], LANES - 1, 1), pltpu.roll(pair[1], LANES - 1, 1)
    return jnp.where(last, high, low), jnp.where(last, 0.0, high)


def z_down(pair):
    first = iota(pair[0].shape, 1) == 0
    low, high = pltpu.roll(pair[0], 1, 1), pltpu.roll(pair[1], 1, 1)
    return jnp.where(first, 0.0, low), jnp.where(first, low, high)


def kernel(
    nx, ny, source, permittivity, frequency, sol, res,
    w, h, gsend, grecv, mat, fx, bx, fy, by, fz, bz, eps, red, row, vecs, coef,
    load_sem, x_send, x_recv, red_send, red_recv,
):
    layers, rows = source.shape[3], source.shape[4]
    depth = source.shape[5]
    halves = depth // LANES
    top = TILE + rows
    ix, iy = lax.axis_index("gx"), lax.axis_index("gy")
    count = nx * ny
    me = ix * ny + iy

    def loads():
        out = []
        for c in range(3):
            for zh in range(halves):
                lanes = pl.ds(zh * LANES, LANES)
                out.append(pltpu.make_async_copy(
                    source.at[0, ORDER[c], :, :, :, lanes],
                    w.at[0, c, :, pl.ds(1, layers), zh, pl.ds(TILE, rows), :],
                    load_sem.at[c * halves + zh]))
        for c in range(3):
            for zh in range(halves):
                lanes = pl.ds(zh * LANES, LANES)
                out.append(pltpu.make_async_copy(
                    permittivity.at[ORDER[c], :, :, lanes], eps.at[c, :, zh],
                    load_sem.at[3 * halves + c * halves + zh]))
        return out

    for copy in loads():
        copy.start()

    zero = jnp.zeros((TILE, LANES), f32)

    def clear(k, carry):
        @pl.when(iy == 0)
        def _():
            for c in range(3):
                for ri in range(2):
                    for x in range(1, layers + 2):
                        for zh in range(halves):
                            w[k, c, ri, x, zh, pl.ds(0, TILE), :] = zero

        @pl.when(iy == ny - 1)
        def _():
            for ri in range(2):
                for zh in range(halves):
                    for c in (CX, CZ):
                        for x in range(1, layers + 1):
                            w[k, c, ri, x, zh, pl.ds(top, TILE), :] = zero

        @pl.when((iy == ny - 1) | (ix == 0))
        def _():
            for ri in range(2):
                for zh in range(halves):
                    w[k, CX, ri, 0, zh, pl.ds(top, TILE), :] = zero

        @pl.when(ix == 0)
        def _():
            for c in range(2):
                for ri in range(2):
                    for zh in range(halves):
                        grecv[k, c, ri, zh] = jnp.zeros((rows, LANES), f32)

        @pl.when(ix == nx - 1)
        def _():
            for c in (CZ, CY):
                for ri in range(2):
                    for zh in range(halves):
                        w[k, c, ri, layers + 1, zh] = jnp.zeros((rows + 2 * TILE, LANES), f32)

        return carry

    lax.fori_loop(0, STEPS, clear, 0)

    barrier = pltpu.get_barrier_semaphore()

    def partner(j):
        d = lax.rem(me + j, count)
        return {"gx": d // ny, "gy": lax.rem(d, ny)}

    def greet(j, carry):
        pl.semaphore_signal(barrier, inc=1, device_id=partner(j), device_id_type=pl.DeviceIdType.MESH)
        return carry

    lax.fori_loop(1, count, greet, 0)

    freq = jnp.full((1, LANES), frequency[0], f32)

    def put(ref, index, pair):
        ref[index + (0,)] = pair[0]
        ref[index + (1,)] = pair[1]

    for x in range(layers + 1):
        point = jnp.full((1, LANES), (ix * layers + (x - 1)).astype(f32), f32)
        exists = jnp.where((ix > 0) | (x > 0), 1.0, 0.0)
        put(fx, (x,), cscale(stretch(point + 0.5, float(nx * layers), freq), exists))
        put(bx, (x,), stretch(point, float(nx * layers), freq))
    freq_rows = jnp.full((top, LANES), frequency[0], f32)
    place = iota((top, LANES), 0) - TILE
    point = (place + iy * rows).astype(f32)
    exists = jnp.where((iy > 0) | (place >= 0), 1.0, 0.0)
    put(fy, (), cscale(stretch(point + 0.5, float(ny * rows), freq_rows), exists))
    put(by, (), stretch(point, float(ny * rows), freq_rows))
    for zh in range(halves):
        point = (iota((1, LANES), 1) + zh * LANES).astype(f32)
        put(fz, (zh,), stretch(point + 0.5, float(depth), freq))
        put(bz, (zh,), stretch(point, float(depth), freq))

    def factor(ref, index, take=slice(None)):
        return ref[index + (0, take)], ref[index + (1, take)]

    both = range(halves)

    def field(ref, lead, x, r):
        return [tuple(ref[lead + (ri, x, zh, pl.ds(r, TILE))] for ri in range(2)) for zh in both]

    def shifted(values, shift):
        parts = [shift([values[zh][ri] for zh in both]) for ri in range(2)]
        return [(parts[0][zh], parts[1][zh]) for zh in both]

    def magnetic(k, x, r, ghost=False):
        ex, ez, ey = (field(w, (k, c), x, r) for c in (CX, CZ, CY))
        ez_y, ex_y = (field(w, (k, c), x, r + 1) for c in (CZ, CX))
        ey_x = field(w, (k, CY), x + 1, r)
        ey_z = shifted(ey, z_up)
        fyr, fxr = factor(fy, (), pl.ds(r, TILE)), factor(fx, (x,))
        if not ghost:
            ez_x = field(w, (k, CZ), x + 1, r)
            ex_z = shifted(ex, z_up)
        for zh in both:
            fzr = factor(fz, (zh,))
            hx = csub(cmul(csub(ez_y[zh], ez[zh]), fyr), cmul(csub(ey_z[zh], ey[zh]), fzr))
            hz = csub(cmul(csub(ey_x[zh], ey[zh]), fxr), cmul(csub(ex_y[zh], ex[zh]), fyr))
            for ri in range(2):
                h[CX, ri, x, zh, pl.ds(r, TILE)] = hx[ri]
                h[CZ, ri, x, zh, pl.ds(r, TILE)] = hz[ri]
            if not ghost:
                hy = csub(cmul(csub(ex_z[zh], ex[zh]), fzr), cmul(csub(ez_x[zh], ez[zh]), fxr))
                for ri in range(2):
                    h[CY, ri, x, zh, pl.ds(r, TILE)] = hy[ri]

    def magnetic_layer(k, x):
        for r in range(0, top, TILE):
            magnetic(k, x, r, r == 0)

    def magnetic_below(k):
        for r in range(TILE, top, TILE):
            ez, ey = field(w, (k, CZ), 1, r), field(w, (k, CY), 1, r)
            fxr = factor(fx, (0,))
            for zh in both:
                gy = tuple(grecv[k, 0, ri, zh, pl.ds(r - TILE, TILE)] for ri in range(2))
                gz = tuple(grecv[k, 1, ri, zh, pl.ds(r - TILE, TILE)] for ri in range(2))
                hy = csub(gy, cmul(fxr, ez[zh]))
                hz = cadd(gz, cmul(fxr, ey[zh]))
                if r == top - TILE:
                    end = iota((TILE, LANES), 0) == TILE - 1
                    beyond = tuple(
                        jnp.where(end, pltpu.roll(w[k, CX, ri, 0, zh, pl.ds(top, TILE)], TILE - 1, 0), 0.0)
                        for ri in range(2))
                    hz = csub(hz, cmul(factor(fy, (), pl.ds(r, TILE)), beyond))
                for ri in range(2):
                    h[CY, ri, 0, zh, pl.ds(r, TILE)] = hy[ri]
                    h[CZ, ri, 0, zh, pl.ds(r, TILE)] = hz[ri]

    def electric_layer(k, x):
        for r in range(TILE, top, TILE):
            hx, hz, hy = (field(h, (c,), x, r) for c in (CX, CZ, CY))
            hz_y, hx_y = field(h, (CZ,), x, r - 1), field(h, (CX,), x, r - 1)
            hz_x, hy_x = field(h, (CZ,), x - 1, r), field(h, (CY,), x - 1, r)
            hy_z, hx_z = shifted(hy, z_down), shifted(hx, z_down)
            byr, bxr = factor(by, (), pl.ds(r, TILE)), factor(bx, (x,))
            for zh in both:
                bzr = factor(bz, (zh,))
                out = {
                    CX: csub(cmul(csub(hz[zh], hz_y[zh]), byr), cmul(csub(hy[zh], hy_z[zh]), bzr)),
                    CY: csub(cmul(csub(hx[zh], hx_z[zh]), bzr), cmul(csub(hz[zh], hz_x[zh]), bxr)),
                    CZ: csub(cmul(csub(hy[zh], hy_x[zh]), bxr), cmul(csub(hx[zh], hx_y[zh]), byr)),
                }
                for c in range(3):
                    m = mat[c, x - 1, zh, pl.ds(r - TILE, TILE)]
                    for ri in range(2):
                        old = w[k, c, ri, x, zh, pl.ds(r, TILE)]
                        w[k + 1, c, ri, x, zh, pl.ds(r, TILE)] = out[c][ri] - m * old

    def upward(k):
        x = layers
        for r in range(TILE, top, TILE):
            ex, ez, ey = (field(w, (k, c), x, r) for c in (CX, CZ, CY))
            if r + TILE < top:
                ex_y = field(w, (k, CX), x, r + 1)
            else:
                end = iota((TILE, LANES), 0) == TILE - 1
                ex_y = [tuple(jnp.where(end, 0.0, pltpu.roll(part, TILE - 1, 0)) for part in v) for v in ex]
            ex_z = shifted(ex, z_up)
            fyr, fxr = factor(fy, (), pl.ds(r, TILE)), factor(fx, (x,))
            for zh in both:
                fzr = factor(fz, (zh,))
                gy = cadd(cmul(csub(ex_z[zh], ex[zh]), fzr), cmul(ez[zh], fxr))
                gz = csub(cneg(cmul(ey[zh], fxr)), cmul(csub(ex_y[zh], ex[zh]), fyr))
                for ri in range(2):
                    gsend[k, 0, ri, zh, pl.ds(r - TILE, TILE)] = gy[ri]
                    gsend[k, 1, ri, zh, pl.ds(r - TILE, TILE)] = gz[ri]

    def remote(k, kind, src, dst, device):
        return pltpu.make_async_remote_copy(
            src_ref=src, dst_ref=dst, send_sem=x_send.at[k, kind], recv_sem=x_recv.at[k, kind],
            device_id=device, device_id_type=pl.DeviceIdType.MESH)

    own = pl.ds(TILE, rows)
    other = 1 - iy

    def down(k):
        return remote(k, 0, w.at[k, pl.ds(CZ, 2), :, 1, :, own], w.at[k, pl.ds(CZ, 2), :, layers + 1, :, own],
                      {"gx": ix - 1, "gy": iy})

    def up(k):
        return remote(k, 1, gsend.at[k], grecv.at[k], {"gx": ix + 1, "gy": iy})

    edge = pl.multiple_of(jnp.where(iy == 0, rows, TILE), TILE)
    ghost = pl.multiple_of(jnp.where(iy == 0, 0, top), TILE)

    def across(k):
        inner = pl.ds(1, layers)
        return remote(k, 2, w.at[k, :, :, inner, :, pl.ds(edge, TILE)], w.at[k, :, :, inner, :, pl.ds(ghost, TILE)],
                      {"gx": ix, "gy": other})

    corner_c = jnp.where(iy == 0, CY, CX)
    corner_from = jnp.where(iy == 0, 1, layers)
    corner_to = jnp.where(iy == 0, layers + 1, 0)
    corner_ix = jnp.where(iy == 0, ix - 1, ix + 1)

    def corner(k):
        return remote(k, 3, w.at[k, corner_c, :, corner_from, :, pl.ds(edge, TILE)],
                      w.at[k, corner_c, :, corner_to, :, pl.ds(ghost, TILE)], {"gx": corner_ix, "gy": other})

    has_low, has_high = ix > 0, ix < nx - 1
    sends_corner = jnp.where(iy == 0, ix > 0, ix < nx - 1)
    gets_corner = jnp.where(iy == 0, ix > 0, ix < nx - 1)

    def start_if(condition, copy):
        @pl.when(condition)
        def _():
            copy.start()

    def wait_recv_if(condition, copy):
        @pl.when(condition)
        def _():
            copy.wait_recv()

    lane8 = iota((TILE, LANES), 1)

    def get_coef(i):
        return coef[2 * i], coef[2 * i + 1]

    def reduce_and_send(rnd, accumulators):
        line = jnp.zeros((TILE, LANES), f32)
        for i, acc in enumerate(accumulators):
            line = line + jnp.where(lane8 == i, jnp.sum(acc, axis=1, keepdims=True), 0.0)
        mine = jnp.sum(line, axis=0, keepdims=True)
        row[rnd] = mine
        red[rnd, me] = mine

        def send(i, carry):
            off = (i + 1) // 2
            j = jnp.where(lax.rem(i, 2) == 1, count // 2 + off, count // 2 - off)
            pltpu.make_async_remote_copy(
                src_ref=row.at[rnd], dst_ref=red.at[rnd, me], send_sem=red_send.at[rnd], recv_sem=red_recv.at[rnd],
                device_id=partner(j), device_id_type=pl.DeviceIdType.MESH).start()
            return carry

        lax.fori_loop(0, count - 1, send, 0)

    def bulk(rnd):
        block = red.at[rnd, pl.ds(0, count - 1)]
        return pltpu.make_async_remote_copy(
            src_ref=block, dst_ref=block, send_sem=red_send.at[rnd], recv_sem=red_recv.at[rnd],
            device_id=partner(1), device_id_type=pl.DeviceIdType.MESH)

    def reduced(rnd):
        bulk(rnd).wait_recv()
        parts = [red[rnd, d] for d in range(count)]
        while len(parts) > 1:
            parts = [a + b for a, b in zip(parts[::2], parts[1::2])]
        line = jnp.broadcast_to(parts[0], (TILE, LANES))
        return [
            jnp.broadcast_to(jnp.sum(jnp.where(lane8 == i, line, 0.0), axis=1, keepdims=True), (TILE, LANES))
            for i in range(VALUES)
        ]

    def scalars(values, rho):
        pair = lambda i: (values[i], values[i + 1])
        sv, sy, sz, yr, yv, zr, zv, yz = (pair(2 * i) for i in range(8))
        yy, zz = values[16], values[17]
        if rho is None:
            rho = (values[18], jnp.zeros_like(values[18]))
        alpha = cdiv(rho, sv)
        square = alpha[0] * alpha[0] + alpha[1] * alpha[1]
        tm = cadd(csub(csub(yr, cmul(alpha, yv)), cmul(conj(alpha), zr)), cscale(zv, square))
        cross = alpha[0] * yz[0] - alpha[1] * yz[1]
        tt = yy - 2.0 * cross + square * zz
        weight = (tm[0] / tt, tm[1] / tt)
        rho_next = cneg(cmul(weight, csub(sy, cmul(alpha, sz))))
        return rho, alpha, weight, rho_next

    def products(s, r, v, y, z):
        dot = lambda a, b: (a[0] * b[0] + a[1] * b[1], a[0] * b[1] - a[1] * b[0])
        norm = lambda a: a[0] * a[0] + a[1] * a[1]
        out = []
        for a, b in ((s, v), (s, y), (s, z), (y, r), (y, v), (z, r), (z, v), (y, z)):
            out += dot(a, b)
        return out + [norm(y), norm(z), norm(s)]

    def block(k, c, x, zh, r):
        return w[k, c, 0, x, zh, pl.ds(r, TILE)], w[k, c, 1, x, zh, pl.ds(r, TILE)]

    def over_blocks(body, carry):
        def at_row(c, x, zh, t, carry):
            return body(c, x, zh, pl.multiple_of(t * TILE + TILE, TILE), carry)

        tiles = rows // TILE

        def step(i, carry):
            t, q = lax.rem(i, tiles), i // tiles
            x, c = lax.rem(q, layers) + 1, q // layers
            for zh in both:
                carry = at_row(c, x, zh, t, carry)
            return carry

        return lax.fori_loop(0, 3 * layers * tiles, step, carry)

    def combine(coefs, basis):
        total = None
        for c, b in zip(coefs, basis):
            if c is None:
                continue
            term = cmul(c, b)
            total = term if total is None else cadd(total, term)
        return total

    def save(base, values):
        for i, v in enumerate(values):
            coef[2 * (base + i)], coef[2 * (base + i) + 1] = v

    def load(base, n):
        return [get_coef(base + i) for i in range(n)]

    R0, P0, X0, RHO = 0, 5, 10, 14
    zero_pair = (zero, zero)
    one_pair = (jnp.ones((TILE, LANES), f32), zero)

    def shift(a):
        return [None] + list(a)

    def minus(a, b, factor_):
        n = max(len(a), len(b))
        out = []
        for i in range(n):
            left = a[i] if i < len(a) else None
            right = b[i] if i < len(b) else None
            right = None if right is None else cmul(factor_, right)
            if left is None and right is None:
                out.append(None)
            elif right is None:
                out.append(left)
            elif left is None:
                out.append(cneg(right))
            else:
                out.append(csub(left, right))
        return out

    def advance(it):
        values = reduced(it)
        if it == 0:
            r, p, x = [one_pair], [one_pair], []
            rho, alpha, weight, rho_next = scalars(values, None)
        else:
            n = 2 * it + 1
            r, p, x = load(R0, n), load(P0, n), load(X0, n - 1)
            rho, alpha, weight, rho_next = scalars(values, get_coef(RHO))
        v = shift(p)
        m = minus(r, v, alpha)
        t = shift(m)
        x = minus(x, p, cneg(alpha))
        x = minus(x, m, cneg(weight))
        r_next = minus(m, t, weight)
        beta = cmul(cdiv(rho_next, rho), cdiv(alpha, weight))
        p_next = minus(r_next, minus(p, v, weight), cneg(beta))
        save(R0, r_next)
        save(P0, p_next)
        save(X0, x)
        save(RHO, [rho_next])

    def gather_products(it):
        n = 2 * it + 1

        def body(c, x, zh, r_, carry):
            basis = [block(k, c, x, zh, r_) for k in range(2 * it + 3)]
            if it == 0:
                r, v, y, z = basis[0], basis[1], basis[1], basis[2]
            else:
                rc, pc = load(R0, n), load(P0, n)
                r = combine(rc, basis)
                v, y = combine(pc, basis[1:]), combine(rc, basis[1:])
                z = combine(pc, basis[2:])
            if it == ITERS - 1:
                for i, value in enumerate((r, v, y, z)):
                    for ri in range(2):
                        vecs[i, c, ri, x - 1, zh, pl.ds(r_ - TILE, TILE)] = value[ri]
            return [a + b for a, b in zip(carry, products(basis[0], r, v, y, z))]

        totals = over_blocks(body, [jnp.zeros((TILE, LANES), f32)] * VALUES)
        reduce_and_send(it, totals)

    def send_layer_low(k):
        start_if(has_low, down(k))

    def send_rest(k):
        upward(k)
        start_if(has_high, up(k))
        across(k).start()
        start_if(sends_corner, corner(k))

    pl.semaphore_wait(barrier, count - 1)
    for copy in loads():
        copy.wait()
    send_layer_low(0)
    send_rest(0)
    for c in range(3):
        for x in range(layers):
            for zh in both:
                mat[c, x, zh] = (freq * freq) * eps[c, x, zh]

    def step(k, carry):
        @pl.when(k == 2)
        def _():
            gather_products(0)

        @pl.when(k == 4)
        def _():
            advance(0)
            gather_products(1)

        across(k).wait_recv()
        for x in range(1, layers):
            magnetic_layer(k, x)
        for x in range(2, layers):
            electric_layer(k, x)
        wait_recv_if(has_low, up(k))
        wait_recv_if(gets_corner, corner(k))
        magnetic_below(k)
        electric_layer(k, 1)

        @pl.when(k + 1 < STEPS)
        def _():
            send_layer_low(k + 1)

        wait_recv_if(has_high, down(k))
        magnetic_layer(k, layers)
        electric_layer(k, layers)

        @pl.when(k + 1 < STEPS)
        def _():
            send_rest(k + 1)

        return carry

    lax.fori_loop(0, STEPS, step, 0)
    advance(1)
    gather_products(2)

    n = 2 * ITERS - 1

    def partial(c, x, zh, r_, carry):
        basis = [block(k, c, x, zh, r_) for k in range(n)]
        xs, ps = combine(load(X0, n - 1), basis), combine(load(P0, n), basis)
        for ri in range(2):
            vecs[4, c, ri, x - 1, zh, pl.ds(r_ - TILE, TILE)] = xs[ri]
            vecs[5, c, ri, x - 1, zh, pl.ds(r_ - TILE, TILE)] = ps[ri]
        return carry

    over_blocks(partial, 0)

    def finish_sends(k, carry):
        @pl.when(has_low)
        def _():
            down(k).wait_send()

        @pl.when(has_high)
        def _():
            up(k).wait_send()

        across(k).wait_send()

        @pl.when(sends_corner)
        def _():
            corner(k).wait_send()

        return carry

    lax.fori_loop(0, STEPS, finish_sends, 0)
    for rnd in range(ITERS - 1):
        bulk(rnd).wait_send()

    values = reduced(ITERS - 1)
    rho, alpha, weight, _ = scalars(values, get_coef(RHO))
    both_factors = cmul(alpha, weight)

    for c in range(3):
        def write(i, carry):
            t, x = lax.rem(i, rows // TILE), i // (rows // TILE)
            r_ = pl.multiple_of(t * TILE, TILE)
            for zh in both:
                r, v, y, z, xs, ps = (
                    tuple(vecs[q, c, ri, x, zh, pl.ds(r_, TILE)] for ri in range(2)) for q in range(6))
                new_x = cadd(xs, cadd(cmul(alpha, ps), csub(cmul(weight, r), cmul(both_factors, v))))
                new_r = cadd(csub(csub(r, cmul(alpha, v)), cmul(weight, y)), cmul(both_factors, z))
                for ri in range(2):
                    sol[0, ORDER[c], ri, x, pl.ds(r_, TILE), pl.ds(zh * LANES, LANES)] = new_x[ri]
                    res[0, ORDER[c], ri, x, pl.ds(r_, TILE), pl.ds(zh * LANES, LANES)] = new_r[ri]
            return carry

        lax.fori_loop(0, layers * (rows // TILE), write, 0)
    bulk(ITERS - 1).wait_send()


def solution(mesh):
    nx, ny = mesh.shape["gx"], mesh.shape["gy"]

    def body(source, permittivity, frequency):
        layers, rows, depth = source.shape[3:]
        halves = depth // LANES
        vmem = lambda *shape: pltpu.VMEM(shape, f32)
        return pl.pallas_call(
            functools.partial(kernel, nx, ny),
            out_shape=(jax.ShapeDtypeStruct(source.shape, f32),) * 2,
            in_specs=[
                pl.BlockSpec(memory_space=pl.ANY),
                pl.BlockSpec(memory_space=pl.ANY),
                pl.BlockSpec(memory_space=pltpu.SMEM),
            ],
            out_specs=(pl.BlockSpec(memory_space=pltpu.VMEM),) * 2,
            scratch_shapes=[
                vmem(STEPS + 1, 3, 2, layers + 2, halves, rows + 2 * TILE, LANES),
                vmem(3, 2, layers + 1, halves, rows + TILE, LANES),
                vmem(STEPS, 2, 2, halves, rows, LANES),
                vmem(STEPS, 2, 2, halves, rows, LANES),
                vmem(3, layers, halves, rows, LANES),
                vmem(layers + 1, 2, 1, LANES),
                vmem(layers + 1, 2, 1, LANES),
                vmem(2, rows + TILE, LANES),
                vmem(2, rows + TILE, LANES),
                vmem(halves, 2, 1, LANES),
                vmem(halves, 2, 1, LANES),
                vmem(3, layers, halves, rows, LANES),
                vmem(ITERS, nx * ny, 1, LANES),
                vmem(ITERS, 1, LANES),
                vmem(6, 3, 2, layers, halves, rows, LANES),
                vmem(30, TILE, LANES),
                pltpu.SemaphoreType.DMA((6 * halves,)),
                pltpu.SemaphoreType.DMA((STEPS, 4)),
                pltpu.SemaphoreType.DMA((STEPS, 4)),
                pltpu.SemaphoreType.DMA((ITERS,)),
                pltpu.SemaphoreType.DMA((ITERS,)),
            ],
            compiler_params=pltpu.CompilerParams(
                collective_id=0, has_side_effects=True, vmem_limit_bytes=48 * 1024 * 1024
            ),
        )(source, permittivity, frequency)

    placed = P("groups", None, None, "gx", "gy", None)
    return jax.shard_map(
        body,
        mesh=mesh,
        in_specs=(placed, P("groups", "gx", "gy", None), P()),
        out_specs=(placed, placed),
        check_vma=False,
    )
```

time: 428 us -> 70.1 us (0.16)
  starting transfers between devices: 105 us -> 0 us
  between operations: 100 us -> 1.29 us
  waiting for transfers between devices: 89 us -> 0 us
  other arithmetic: 76.9 us -> 0 us
  Pallas kernels: 0 us -> 64.7 us
  local copies, waits for them, and re-layouts: 36.4 us -> 3.88 us
  blocking collectives: 17.5 us -> 0 us
    pallas_call x0 -> x1, Pallas kernels: none -> 64.7 us  [body(): pl.pallas_call(functools.partial(kernel, nx, ny), out_shape=(jax.ShapeDty...]
    ppermute x24 -> x0, starting transfers between devices: 64.3 us -> none  [the longest x12 40.2 us: with_halo(): lax.ppermute(lax.slice_in_dim(block, 0, width, axis=dim), axis, backward)]
    all_to_all x6 -> x0, waiting for transfers between devices: 56.8 us -> none  [sent_to_all(): return lax.all_to_all(copies, axis, split_axis=0, concat_axis=0, tiled=True)]
    all_to_all x6 -> x0, starting transfers between devices: 40.5 us -> none  [sent_to_all(): return lax.all_to_all(copies, axis, split_axis=0, concat_axis=0, tiled=True)]
    sub x77 -> x0, other arithmetic: 38.9 us -> none  [the longest x15 27.6 us: scaled(): real_part = values[:, :, 0] * real_scale - values[:, :, 1] * imag_scale]
    ppermute x24 -> x0, waiting for transfers between devices: 32.1 us -> none  [the longest x12 22 us: with_halo(): lax.ppermute(lax.slice_in_dim(block, 0, width, axis=dim), axis, backward)]
    all_to_all x1 -> x0, blocking collectives: 17.5 us -> none  [sent_to_all(): return lax.all_to_all(copies, axis, split_axis=0, concat_axis=0, tiled=True)]
    slice x40 -> x0, local copies, waits for them, and re-layouts: 17.2 us -> none  [the longest x4 4.27 us: complex_times(): other[0]]
  transfers between devices with their start and end apart: 30 -> 0, of which waited for: 22 -> 0; matrix products, arithmetic and copies ran while one was open for 3% -> 0% of each run, Pallas kernels for 0% -> 0%
where the time goes in v1:
time: 70.1 us; the launch traced here: 69.9 us
  Pallas kernels  64.7 us (92%)
  local copies, waits for them, and re-layouts  3.88 us (6%)
  between operations  1.29 us (2%)
    pallas_call x1, Pallas kernels, body(): pl.pallas_call(functools.partial(kernel, nx, ny), out_shape=(jax.ShapeDty...  64.7 us
    unnamed x6, local copies, waits for them, and re-layouts  3.88 us

profile of v1, /device:TPU:69, one launch (start us, length us, event | category | flops | bytes accessed | tf_op | source)
XLA Modules:
  0.0 69.9 jit_solution(1512141750071178557)
XLA Ops:
  1.3 0.0 copy-start
  1.3 1.1 %copy-done = f32[1,3,2,4,32,256]{5,4,3,2,1,0:T(8,128)S(1)} copy-done((f32[1,3,2,4,32,256]{5,4,3,2,1,0:T(8,128)S(1)}, f32[1,3,2,4,32,256]{5,4,3,2,1,0:T(8,128)}, u32[]{:S(2)}) %copy-start) | copy-done | bytes 786456
  2.4 0.0 copy-start.1
  2.4 1.0 %copy-done.1 = f32[3,4,32,256]{3,2,1,0:T(8,128)S(1)} copy-done((f32[3,4,32,256]{3,2,1,0:T(8,128)S(1)}, f32[3,4,32,256]{3,2,1,0:T(8,128)}, u32[]{:S(2)}) %copy-start.1) | copy-done | bytes 393240
  3.4 64.7 %shard_map.50 = (f32[1,3,2,4,32,256]{5,4,3,2,1,0:T(8,128)S(1)}, f32[1,3,2,4,32,256]{5,4,3,2,1,0:T(8,128)S(1)}) custom-call(f32[1,3,2,4,32,256]{5,4,3,2,1,0:T(8,128)S(1)} %copy-done, f32[3,4,32,256]{3,2,1,0:T(8,128)S(1)} %copy-done.1, f32[1]{0:T(128)S(6)} %copy.7.frequency), custom_call_target="tpu_custom_call" | custom-call | tf_op jit(solution)/shard_map/pallas_call | solution.py:609
  68.1 0.9 %copy.8 = f32[1,3,2,4,32,256]{5,4,3,2,1,0:T(8,128)} copy(f32[1,3,2,4,32,256]{5,4,3,2,1,0:T(8,128)S(1)} %get-tuple-element.4) | data formatting | bytes 1572864
  69.0 0.9 %copy.9 = f32[1,3,2,4,32,256]{5,4,3,2,1,0:T(8,128)} copy(f32[1,3,2,4,32,256]{5,4,3,2,1,0:T(8,128)S(1)} %get-tuple-element.5) | data formatting | bytes 1572864
Async XLA Ops:
  1.3 1.1 %copy-start = (f32[1,3,2,4,32,256]{5,4,3,2,1,0:T(8,128)S(1)}, f32[1,3,2,4,32,256]{5,4,3,2,1,0:T(8,128)}, u32[]{:S(2)}) copy-start(f32[1,3,2,4,32,256]{5,4,3,2,1,0:T(8,128)} %source.1) | copy-start | bytes 2359300
  2.4 1.0 %copy-start.1 = (f32[3,4,32,256]{3,2,1,0:T(8,128)S(1)}, f32[3,4,32,256]{3,2,1,0:T(8,128)}, u32[]{:S(2)}) copy-start(f32[3,4,32,256]{3,2,1,0:T(8,128)} %permittivity.1) | copy-start | bytes 1179652

commit v2 on v1

--- a/solution.py
+++ b/solution.py
@@ -16,6 +16,7 @@
 LANES = 128
 TILE = 8
 VALUES = 19
+TOKENS = 3
 
 f32 = jnp.float32
 
@@ -75,7 +76,7 @@
 def kernel(
     nx, ny, source, permittivity, frequency, sol, res,
     w, h, gsend, grecv, mat, fx, bx, fy, by, fz, bz, eps, red, row, vecs, coef,
-    load_sem, x_send, x_recv, red_send, red_recv,
+    load_sem, x_send, x_recv, red_send, red_recv, token,
 ):
     layers, rows = source.shape[3], source.shape[4]
     depth = source.shape[5]
@@ -154,11 +155,20 @@
         d = lax.rem(me + j, count)
         return {"gx": d // ny, "gy": lax.rem(d, ny)}
 
-    def greet(j, carry):
-        pl.semaphore_signal(barrier, inc=1, device_id=partner(j), device_id_type=pl.DeviceIdType.MESH)
-        return carry
-
-    lax.fori_loop(1, count, greet, 0)
+    def signal(sem, gx, gy):
+        pl.semaphore_signal(sem, inc=1, device_id={"gx": gx, "gy": gy}, device_id_type=pl.DeviceIdType.MESH)
+
+    def ring(distance):
+        return lax.rem(ix + distance, nx), lax.rem(ix + nx - distance, nx)
+
+    for gx in ring(1):
+        for gy in range(ny):
+            signal(barrier, gx, gy)
+    signal(barrier, ix, 1 - iy)
+
+    def pass_token(index, distance):
+        for gx in ring(distance):
+            signal(token.at[index], gx, iy)
 
     freq = jnp.full((1, LANES), frequency[0], f32)
 
@@ -219,8 +229,8 @@
         for r in range(0, top, TILE):
             magnetic(k, x, r, r == 0)
 
-    def magnetic_below(k):
-        for r in range(TILE, top, TILE):
+    def magnetic_below(k, r):
+        if True:
             ez, ey = field(w, (k, CZ), 1, r), field(w, (k, CY), 1, r)
             fxr = factor(fx, (0,))
             for zh in both:
@@ -240,6 +250,10 @@
 
     def electric_layer(k, x):
         for r in range(TILE, top, TILE):
+            electric(k, x, r)
+
+    def electric(k, x, r):
+        if True:
             hx, hz, hy = (field(h, (c,), x, r) for c in (CX, CZ, CY))
             hz_y, hx_y = field(h, (CZ,), x, r - 1), field(h, (CX,), x, r - 1)
             hz_x, hy_x = field(h, (CZ,), x - 1, r), field(h, (CY,), x - 1, r)
@@ -258,9 +272,9 @@
                         old = w[k, c, ri, x, zh, pl.ds(r, TILE)]
                         w[k + 1, c, ri, x, zh, pl.ds(r, TILE)] = out[c][ri] - m * old
 
-    def upward(k):
+    def upward(k, r):
         x = layers
-        for r in range(TILE, top, TILE):
+        if True:
             ex, ez, ey = (field(w, (k, c), x, r) for c in (CX, CZ, CY))
             if r + TILE < top:
                 ex_y = field(w, (k, CX), x, r + 1)
@@ -282,22 +296,24 @@
             src_ref=src, dst_ref=dst, send_sem=x_send.at[k, kind], recv_sem=x_recv.at[k, kind],
             device_id=device, device_id_type=pl.DeviceIdType.MESH)
 
-    own = pl.ds(TILE, rows)
     other = 1 - iy
-
-    def down(k):
-        return remote(k, 0, w.at[k, pl.ds(CZ, 2), :, 1, :, own], w.at[k, pl.ds(CZ, 2), :, layers + 1, :, own],
+    tiles = rows // TILE
+
+    def down(k, t):
+        part = pl.ds(TILE + t * TILE, TILE)
+        return remote(k, t, w.at[k, pl.ds(CZ, 2), :, 1, :, part], w.at[k, pl.ds(CZ, 2), :, layers + 1, :, part],
                       {"gx": ix - 1, "gy": iy})
 
-    def up(k):
-        return remote(k, 1, gsend.at[k], grecv.at[k], {"gx": ix + 1, "gy": iy})
+    def up(k, t):
+        part = pl.ds(t * TILE, TILE)
+        return remote(k, tiles + t, gsend.at[k, :, :, :, part], grecv.at[k, :, :, :, part], {"gx": ix + 1, "gy": iy})
 
     edge = pl.multiple_of(jnp.where(iy == 0, rows, TILE), TILE)
     ghost = pl.multiple_of(jnp.where(iy == 0, 0, top), TILE)
 
     def across(k):
         inner = pl.ds(1, layers)
-        return remote(k, 2, w.at[k, :, :, inner, :, pl.ds(edge, TILE)], w.at[k, :, :, inner, :, pl.ds(ghost, TILE)],
+        return remote(k, 2 * tiles, w.at[k, :, :, inner, :, pl.ds(edge, TILE)], w.at[k, :, :, inner, :, pl.ds(ghost, TILE)],
                       {"gx": ix, "gy": other})
 
     corner_c = jnp.where(iy == 0, CY, CX)
@@ -306,7 +322,7 @@
     corner_ix = jnp.where(iy == 0, ix - 1, ix + 1)
 
     def corner(k):
-        return remote(k, 3, w.at[k, corner_c, :, corner_from, :, pl.ds(edge, TILE)],
+        return remote(k, 2 * tiles + 1, w.at[k, corner_c, :, corner_from, :, pl.ds(edge, TILE)],
                       w.at[k, corner_c, :, corner_to, :, pl.ds(ghost, TILE)], {"gx": corner_ix, "gy": other})
 
     has_low, has_high = ix > 0, ix < nx - 1
@@ -487,28 +503,31 @@
         totals = over_blocks(body, [jnp.zeros((TILE, LANES), f32)] * VALUES)
         reduce_and_send(it, totals)
 
-    def send_layer_low(k):
-        start_if(has_low, down(k))
-
-    def send_rest(k):
-        upward(k)
-        start_if(has_high, up(k))
-        across(k).start()
-        start_if(sends_corner, corner(k))
-
-    pl.semaphore_wait(barrier, count - 1)
+    pl.semaphore_wait(barrier, 2 * ny + 1)
+    pass_token(0, 1)
     for copy in loads():
         copy.wait()
-    send_layer_low(0)
-    send_rest(0)
+    for t in range(tiles):
+        start_if(has_low, down(0, t))
+    for t in range(tiles):
+        upward(0, TILE + t * TILE)
+        start_if(has_high, up(0, t))
+    across(0).start()
+    start_if(sends_corner, corner(0))
     for c in range(3):
         for x in range(layers):
             for zh in both:
                 mat[c, x, zh] = (freq * freq) * eps[c, x, zh]
 
     def step(k, carry):
+        @pl.when(k < TOKENS - 1)
+        def _():
+            pl.semaphore_wait(token.at[k], 2)
+            pass_token(k + 1, 2 * (k + 1))
+
         @pl.when(k == 2)
         def _():
+            pl.semaphore_wait(token.at[TOKENS - 1], 2)
             gather_products(0)
 
         @pl.when(k == 4)
@@ -521,23 +540,37 @@
             magnetic_layer(k, x)
         for x in range(2, layers):
             electric_layer(k, x)
-        wait_recv_if(has_low, up(k))
-        wait_recv_if(gets_corner, corner(k))
-        magnetic_below(k)
-        electric_layer(k, 1)
-
-        @pl.when(k + 1 < STEPS)
-        def _():
-            send_layer_low(k + 1)
-
-        wait_recv_if(has_high, down(k))
-        magnetic_layer(k, layers)
-        electric_layer(k, layers)
-
-        @pl.when(k + 1 < STEPS)
-        def _():
-            send_rest(k + 1)
-
+        more = k + 1 < STEPS
+        lower_core, upper_core = iy == 0, iy == ny - 1
+        for t in range(tiles):
+            r = TILE + t * TILE
+            wait_recv_if(has_low, up(k, t))
+            if t == tiles - 1:
+                wait_recv_if(lower_core & gets_corner, corner(k))
+            magnetic_below(k, r)
+            electric(k, 1, r)
+            start_if(more & has_low, down(k + 1, t))
+            wait_recv_if(has_high, down(k, t))
+            if t == 0:
+                wait_recv_if(upper_core & gets_corner, corner(k))
+                magnetic(k, layers, 0, True)
+            magnetic(k, layers, r)
+            electric(k, layers, r)
+            if t == 0:
+                start_if(more & upper_core & sends_corner, corner(k + 1))
+                start_if(more & upper_core, across(k + 1))
+            else:
+                @pl.when(more)
+                def _():
+                    upward(k + 1, r - TILE)
+                start_if(more & has_high, up(k + 1, t - 1))
+
+        @pl.when(more)
+        def _():
+            upward(k + 1, top - TILE)
+        start_if(more & has_high, up(k + 1, tiles - 1))
+        start_if(more & lower_core & sends_corner, corner(k + 1))
+        start_if(more & lower_core, across(k + 1))
         return carry
 
     lax.fori_loop(0, STEPS, step, 0)
@@ -557,13 +590,14 @@
     over_blocks(partial, 0)
 
     def finish_sends(k, carry):
-        @pl.when(has_low)
-        def _():
-            down(k).wait_send()
-
-        @pl.when(has_high)
-        def _():
-            up(k).wait_send()
+        for t in range(tiles):
+            @pl.when(has_low)
+            def _():
+                down(k, t).wait_send()
+
+            @pl.when(has_high)
+            def _():
+                up(k, t).wait_send()
 
         across(k).wait_send()
 
@@ -610,8 +644,8 @@
             functools.partial(kernel, nx, ny),
             out_shape=(jax.ShapeDtypeStruct(source.shape, f32),) * 2,
             in_specs=[
-                pl.BlockSpec(memory_space=pl.ANY),
-                pl.BlockSpec(memory_space=pl.ANY),
+                pl.BlockSpec(memory_space=pltpu.HBM),
+                pl.BlockSpec(memory_space=pltpu.HBM),
                 pl.BlockSpec(memory_space=pltpu.SMEM),
             ],
             out_specs=(pl.BlockSpec(memory_space=pltpu.VMEM),) * 2,
@@ -633,10 +667,11 @@
                 vmem(6, 3, 2, layers, halves, rows, LANES),
                 vmem(30, TILE, LANES),
                 pltpu.SemaphoreType.DMA((6 * halves,)),
-                pltpu.SemaphoreType.DMA((STEPS, 4)),
-                pltpu.SemaphoreType.DMA((STEPS, 4)),
+                pltpu.SemaphoreType.DMA((STEPS, 2 * (rows // TILE) + 2)),
+                pltpu.SemaphoreType.DMA((STEPS, 2 * (rows // TILE) + 2)),
                 pltpu.SemaphoreType.DMA((ITERS,)),
                 pltpu.SemaphoreType.DMA((ITERS,)),
+                pltpu.SemaphoreType.REGULAR((TOKENS,)),
             ],
             compiler_params=pltpu.CompilerParams(
                 collective_id=0, has_side_effects=True, vmem_limit_bytes=48 * 1024 * 1024

time: 70.1 us -> 64 us (0.913)
  Pallas kernels: 64.7 us -> 58.7 us
    pallas_call x1, Pallas kernels: 64.7 us -> 58.7 us  [body(): pl.pallas_call(functools.partial(kernel, nx, ny), out_shape=(jax.ShapeDty...]
where the time goes in v2:
time: 64 us; the launch traced here: 63.8 us
  Pallas kernels  58.7 us (92%)
  local copies, waits for them, and re-layouts  3.88 us (6%)
  between operations  1.29 us (2%)
    pallas_call x1, Pallas kernels, body(): pl.pallas_call(functools.partial(kernel, nx, ny), out_shape=(jax.ShapeDty...  58.7 us
    unnamed x6, local copies, waits for them, and re-layouts  3.88 us

profile of v2, /device:TPU:69, one launch (start us, length us, event | category | flops | bytes accessed | tf_op | source)
XLA Modules:
  0.0 63.8 jit_solution(17524348941360629697)
XLA Ops:
  1.3 0.0 copy-start
  1.3 1.1 %copy-done = f32[1,3,2,4,32,256]{5,4,3,2,1,0:T(8,128)S(1)} copy-done((f32[1,3,2,4,32,256]{5,4,3,2,1,0:T(8,128)S(1)}, f32[1,3,2,4,32,256]{5,4,3,2,1,0:T(8,128)}, u32[]{:S(2)}) %copy-start) | copy-done | bytes 786456
  2.4 0.0 copy-start.1
  2.4 1.0 %copy-done.1 = f32[3,4,32,256]{3,2,1,0:T(8,128)S(1)} copy-done((f32[3,4,32,256]{3,2,1,0:T(8,128)S(1)}, f32[3,4,32,256]{3,2,1,0:T(8,128)}, u32[]{:S(2)}) %copy-start.1) | copy-done | bytes 393240
  3.4 58.7 %shard_map.50 = (f32[1,3,2,4,32,256]{5,4,3,2,1,0:T(8,128)S(1)}, f32[1,3,2,4,32,256]{5,4,3,2,1,0:T(8,128)S(1)}) custom-call(f32[1,3,2,4,32,256]{5,4,3,2,1,0:T(8,128)S(1)} %copy-done, f32[3,4,32,256]{3,2,1,0:T(8,128)S(1)} %copy-done.1, f32[1]{0:T(128)S(6)} %copy.7.frequency), custom_call_target="tpu_custom_call" | custom-call | tf_op jit(solution)/shard_map/pallas_call | solution.py:643
  62.1 0.9 %copy.8 = f32[1,3,2,4,32,256]{5,4,3,2,1,0:T(8,128)} copy(f32[1,3,2,4,32,256]{5,4,3,2,1,0:T(8,128)S(1)} %get-tuple-element.4) | data formatting | bytes 1572864
  62.9 0.9 %copy.9 = f32[1,3,2,4,32,256]{5,4,3,2,1,0:T(8,128)} copy(f32[1,3,2,4,32,256]{5,4,3,2,1,0:T(8,128)S(1)} %get-tuple-element.5) | data formatting | bytes 1572864
Async XLA Ops:
  1.3 1.1 %copy-start = (f32[1,3,2,4,32,256]{5,4,3,2,1,0:T(8,128)S(1)}, f32[1,3,2,4,32,256]{5,4,3,2,1,0:T(8,128)}, u32[]{:S(2)}) copy-start(f32[1,3,2,4,32,256]{5,4,3,2,1,0:T(8,128)} %source.1) | copy-start | bytes 2359300
  2.4 1.0 %copy-start.1 = (f32[3,4,32,256]{3,2,1,0:T(8,128)S(1)}, f32[3,4,32,256]{3,2,1,0:T(8,128)}, u32[]{:S(2)}) copy-start(f32[3,4,32,256]{3,2,1,0:T(8,128)} %permittivity.1) | copy-start | bytes 1179652

commit v3 on v2

--- a/solution.py
+++ b/solution.py
@@ -11,11 +11,11 @@
 ITERS = 3
 STRENGTH = 2.0
 STEPS = 2 * ITERS
+PER = 4
 CX, CZ, CY = 0, 1, 2
 ORDER = (0, 2, 1)
 LANES = 128
 TILE = 8
-VALUES = 19
 TOKENS = 3
 
 f32 = jnp.float32
@@ -86,24 +86,41 @@
     count = nx * ny
     me = ix * ny + iy
 
-    def loads():
-        out = []
-        for c in range(3):
-            for zh in range(halves):
-                lanes = pl.ds(zh * LANES, LANES)
-                out.append(pltpu.make_async_copy(
-                    source.at[0, ORDER[c], :, :, :, lanes],
-                    w.at[0, c, :, pl.ds(1, layers), zh, pl.ds(TILE, rows), :],
-                    load_sem.at[c * halves + zh]))
-        for c in range(3):
-            for zh in range(halves):
-                lanes = pl.ds(zh * LANES, LANES)
-                out.append(pltpu.make_async_copy(
-                    permittivity.at[ORDER[c], :, :, lanes], eps.at[c, :, zh],
-                    load_sem.at[3 * halves + c * halves + zh]))
-        return out
-
-    for copy in loads():
+    barrier = pltpu.get_barrier_semaphore()
+
+    def signal(sem, gx, gy):
+        pl.semaphore_signal(sem, inc=1, device_id={"gx": gx, "gy": gy}, device_id_type=pl.DeviceIdType.MESH)
+
+    def ring(distance):
+        return lax.rem(ix + distance, nx), lax.rem(ix + nx - distance, nx)
+
+    for gx in ring(1):
+        for gy in range(ny):
+            signal(barrier, gx, gy)
+    signal(barrier, ix, 1 - iy)
+
+    def pass_token(index, distance):
+        for gx in ring(distance):
+            signal(token.at[index], gx, iy)
+
+    def load_source():
+        return [
+            pltpu.make_async_copy(
+                source.at[0, ORDER[c], :, :, :, pl.ds(zh * LANES, LANES)],
+                w.at[0, c, :, pl.ds(1, layers), zh, pl.ds(TILE, rows), :],
+                load_sem.at[c * halves + zh])
+            for c in range(3) for zh in range(halves)
+        ]
+
+    def load_rest():
+        return [
+            pltpu.make_async_copy(
+                permittivity.at[ORDER[c], :, :, pl.ds(zh * LANES, LANES)], eps.at[c, :, zh],
+                load_sem.at[(3 + c) * halves + zh])
+            for c in range(3) for zh in range(halves)
+        ]
+
+    for copy in load_source() + load_rest():
         copy.start()
 
     zero = jnp.zeros((TILE, LANES), f32)
@@ -148,27 +165,6 @@
         return carry
 
     lax.fori_loop(0, STEPS, clear, 0)
-
-    barrier = pltpu.get_barrier_semaphore()
-
-    def partner(j):
-        d = lax.rem(me + j, count)
-        return {"gx": d // ny, "gy": lax.rem(d, ny)}
-
-    def signal(sem, gx, gy):
-        pl.semaphore_signal(sem, inc=1, device_id={"gx": gx, "gy": gy}, device_id_type=pl.DeviceIdType.MESH)
-
-    def ring(distance):
-        return lax.rem(ix + distance, nx), lax.rem(ix + nx - distance, nx)
-
-    for gx in ring(1):
-        for gy in range(ny):
-            signal(barrier, gx, gy)
-    signal(barrier, ix, 1 - iy)
-
-    def pass_token(index, distance):
-        for gx in ring(distance):
-            signal(token.at[index], gx, iy)
 
     freq = jnp.full((1, LANES), frequency[0], f32)
 
@@ -316,14 +312,16 @@
         return remote(k, 2 * tiles, w.at[k, :, :, inner, :, pl.ds(edge, TILE)], w.at[k, :, :, inner, :, pl.ds(ghost, TILE)],
                       {"gx": ix, "gy": other})
 
+    corner_row = jnp.where(iy == 0, top - 1, TILE)
+    corner_ghost = jnp.where(iy == 0, TILE - 1, top)
     corner_c = jnp.where(iy == 0, CY, CX)
     corner_from = jnp.where(iy == 0, 1, layers)
     corner_to = jnp.where(iy == 0, layers + 1, 0)
     corner_ix = jnp.where(iy == 0, ix - 1, ix + 1)
 
     def corner(k):
-        return remote(k, 2 * tiles + 1, w.at[k, corner_c, :, corner_from, :, pl.ds(edge, TILE)],
-                      w.at[k, corner_c, :, corner_to, :, pl.ds(ghost, TILE)], {"gx": corner_ix, "gy": other})
+        return remote(k, 2 * tiles + 1, w.at[k, corner_c, :, corner_from, :, pl.ds(corner_row, 1)],
+                      w.at[k, corner_c, :, corner_to, :, pl.ds(corner_ghost, 1)], {"gx": corner_ix, "gy": other})
 
     has_low, has_high = ix > 0, ix < nx - 1
     sends_corner = jnp.where(iy == 0, ix > 0, ix < nx - 1)
@@ -334,10 +332,11 @@
         def _():
             copy.start()
 
-    def wait_recv_if(condition, copy):
-        @pl.when(condition)
-        def _():
-            copy.wait_recv()
+    def wait_recv_if(condition, copy, name="wait_x"):
+        with jax.named_scope(name):
+            @pl.when(condition)
+            def _():
+                copy.wait_recv()
 
     lane8 = iota((TILE, LANES), 1)
 
@@ -352,242 +351,374 @@
         row[rnd] = mine
         red[rnd, me] = mine
 
-        def send(i, carry):
-            off = (i + 1) // 2
-            j = jnp.where(lax.rem(i, 2) == 1, count // 2 + off, count // 2 - off)
+        def send(gx, gy):
             pltpu.make_async_remote_copy(
                 src_ref=row.at[rnd], dst_ref=red.at[rnd, me], send_sem=red_send.at[rnd], recv_sem=red_recv.at[rnd],
-                device_id=partner(j), device_id_type=pl.DeviceIdType.MESH).start()
-            return carry
-
-        lax.fori_loop(0, count - 1, send, 0)
+                device_id={"gx": gx, "gy": gy}, device_id_type=pl.DeviceIdType.MESH).start()
+
+        for far in range(nx // 2, 0, -1):
+            above, below = ix + far, ix - far
+            above = jnp.where(above >= nx, above - nx, above)
+            below = jnp.where(below < 0, below + nx, below)
+            for gy in range(ny):
+                send(above, gy)
+                if 2 * far < nx:
+                    send(below, gy)
+        send(ix, 1 - iy)
 
     def bulk(rnd):
         block = red.at[rnd, pl.ds(0, count - 1)]
         return pltpu.make_async_remote_copy(
             src_ref=block, dst_ref=block, send_sem=red_send.at[rnd], recv_sem=red_recv.at[rnd],
-            device_id=partner(1), device_id_type=pl.DeviceIdType.MESH)
-
-    def reduced(rnd):
-        bulk(rnd).wait_recv()
+            device_id={"gx": ix, "gy": other}, device_id_type=pl.DeviceIdType.MESH)
+
+    def reduced(rnd, n):
+        with jax.named_scope(f"wait_reduced_{rnd}"):
+            bulk(rnd).wait_recv()
         parts = [red[rnd, d] for d in range(count)]
         while len(parts) > 1:
             parts = [a + b for a, b in zip(parts[::2], parts[1::2])]
         line = jnp.broadcast_to(parts[0], (TILE, LANES))
         return [
             jnp.broadcast_to(jnp.sum(jnp.where(lane8 == i, line, 0.0), axis=1, keepdims=True), (TILE, LANES))
-            for i in range(VALUES)
+            for i in range(n)
         ]
 
-    def scalars(values, rho):
-        pair = lambda i: (values[i], values[i + 1])
-        sv, sy, sz, yr, yv, zr, zv, yz = (pair(2 * i) for i in range(8))
-        yy, zz = values[16], values[17]
-        if rho is None:
-            rho = (values[18], jnp.zeros_like(values[18]))
+    def dot(a, b):
+        return [a[0] * b[0] + a[1] * b[1], a[0] * b[1] - a[1] * b[0]]
+
+    def norm(a):
+        return [a[0] * a[0] + a[1] * a[1]]
+
+    def block(k, c, x, zh, r):
+        return w[k, c, 0, x, zh, pl.ds(r, TILE)], w[k, c, 1, x, zh, pl.ds(r, TILE)]
+
+    def over_blocks(body, n):
+        per = PER
+
+        def step(i, carry):
+            q = i // (tiles // per)
+            t = lax.rem(i, tiles // per) * per
+            x, c = lax.rem(q, layers) + 1, q // layers
+            for u in range(per):
+                for zh in both:
+                    out = body(c, x, zh, pl.multiple_of((t + u) * TILE + TILE, TILE))
+                    if n:
+                        carry = [a + b for a, b in zip(carry, out)]
+            return carry
+
+        return lax.fori_loop(0, 3 * layers * tiles // per, step, [jnp.zeros((TILE, LANES), f32)] * n)
+
+    def combine(coefs, basis):
+        total = None
+        for c, b in zip(coefs, basis):
+            term = cmul(c, b)
+            total = term if total is None else cadd(total, term)
+        return total
+
+    def save(base, values):
+        for i, v in enumerate(values):
+            coef[2 * (base + i)], coef[2 * (base + i) + 1] = v
+
+    def load(base, n):
+        return [get_coef(base + i) for i in range(n)]
+
+    R0, P0, X0, RHO, ALPHA, WEIGHT, BETA = 0, 5, 10, 14, 15, 16, 17
+    one_pair = (jnp.ones((TILE, LANES), f32), zero)
+
+    def shift(a):
+        return [None] + list(a)
+
+    def plus(a, b, factor_):
+        out = []
+        for i in range(max(len(a), len(b))):
+            left = a[i] if i < len(a) else None
+            right = b[i] if i < len(b) else None
+            right = None if right is None else cmul(factor_, right)
+            out.append(right if left is None else left if right is None else cadd(left, right))
+        return out
+
+    def update(r, p, x, m, alpha, weight, rho, rho_next):
+        x = plus(plus(x, p, alpha), m, weight)
+        r_next = plus(m, shift(m), cneg(weight))
+        beta = cmul(cdiv(rho_next, rho), cdiv(alpha, weight))
+        p_next = plus(r_next, plus(p, shift(p), cneg(weight)), beta)
+        save(R0, r_next)
+        save(P0, p_next)
+        save(X0, x)
+        save(RHO, [rho_next, alpha, weight, beta])
+
+    def gather_early():
+        def body(c, x, zh, r_):
+            a, b = (block(k, c, x, zh, r_) for k in range(2))
+            return dot(a, b) + norm(a) + norm(b)
+
+        for i, total in enumerate(over_blocks(body, 4)):
+            coef[i] = total
+
+    def gather_first():
+        def body(c, x, zh, r_):
+            a, b, d = (block(k, c, x, zh, r_) for k in range(3))
+            return dot(a, d) + dot(b, d) + norm(d)
+
+        late = over_blocks(body, 5)
+        reduce_and_send(0, [coef[0], coef[1]] + late[:4] + [coef[2], coef[3], late[4]])
+
+    def advance_first():
+        values = reduced(0, 9)
+        sv, sz, yz = (tuple(values[2 * i : 2 * i + 2]) for i in range(3))
+        rho, alpha, weight = steps_of(
+            (values[6], zero), sv, conj(sv), (values[7], zero), conj(sz), conj(yz), yz, values[7], values[8])
+        rho_next = cneg(cmul(weight, csub(sv, cmul(alpha, sz))))
+        update([one_pair], [one_pair], [], [one_pair, cneg(alpha)], alpha, weight, rho, rho_next)
+
+    def steps_of(rho, sv, yr, yv, zr, zv, yz, yy, zz):
         alpha = cdiv(rho, sv)
         square = alpha[0] * alpha[0] + alpha[1] * alpha[1]
         tm = cadd(csub(csub(yr, cmul(alpha, yv)), cmul(conj(alpha), zr)), cscale(zv, square))
-        cross = alpha[0] * yz[0] - alpha[1] * yz[1]
-        tt = yy - 2.0 * cross + square * zz
-        weight = (tm[0] / tt, tm[1] / tt)
+        tt = yy - 2.0 * (alpha[0] * yz[0] - alpha[1] * yz[1]) + square * zz
+        return rho, alpha, (tm[0] / tt, tm[1] / tt)
+
+    def products(r, v, y, z, others):
+        out = []
+        for a, b in ((y, r), (y, v), (z, r), (z, v), (y, z)) + others:
+            out += dot(a, b)
+        return out + norm(y) + norm(z)
+
+    def read_products(values, shadow):
+        pairs = [tuple(values[2 * i : 2 * i + 2]) for i in range(5 + shadow)]
+        yr, yv, zr, zv, yz, sv = pairs[:6]
+        yy, zz = values[2 * len(pairs) :][:2]
+        return steps_of(get_coef(RHO), sv, yr, yv, zr, zv, yz, yy, zz), pairs[6:]
+
+    def keep(i, c, x, zh, r_, value):
+        for ri in range(2):
+            vecs[i, c, ri, x - 1, zh, pl.ds(r_ - TILE, TILE)] = value[ri]
+
+    def kept(i, c, x, zh, r_):
+        return tuple(vecs[i, c, ri, x - 1, zh, pl.ds(r_ - TILE, TILE)] for ri in range(2))
+
+    R, V, Y, Z, AY, AZ, AAY, AAZ, XS, PS = range(10)
+
+    def gather_middle():
+        rc, pc = load(R0, 3), load(P0, 3)
+
+        def body(c, x, zh, r_):
+            basis = [block(k, c, x, zh, r_) for k in range(5)]
+            r, v, y, z = combine(rc, basis), combine(pc, basis[1:]), combine(rc, basis[1:]), combine(pc, basis[2:])
+            for i, value in ((R, r), (V, v), (Y, y), (Z, z)):
+                keep(i, c, x, zh, r_, value)
+            return products(r, v, y, z, tuple((basis[0], b) for b in (v, y, z)))
+
+        reduce_and_send(1, over_blocks(body, 18))
+
+    def look_ahead():
+        rc, pc = load(R0, 3), load(P0, 3)
+
+        def body(c, x, zh, r_):
+            basis = [block(k, c, x, zh, r_) for k in range(2, 6)]
+            for i, value in (
+                (AY, combine(rc, basis)), (AZ, combine(pc, basis[1:])),
+                (AAY, combine(rc, basis[1:])), (AAZ, combine(pc, basis[2:])),
+            ):
+                keep(i, c, x, zh, r_, value)
+
+        over_blocks(body, 0)
+
+    def advance_middle():
+        values = reduced(1, 18)
+        (rho, alpha, weight), (sy, sz) = read_products(values, 3)
         rho_next = cneg(cmul(weight, csub(sy, cmul(alpha, sz))))
-        return rho, alpha, weight, rho_next
-
-    def products(s, r, v, y, z):
-        dot = lambda a, b: (a[0] * b[0] + a[1] * b[1], a[0] * b[1] - a[1] * b[0])
-        norm = lambda a: a[0] * a[0] + a[1] * a[1]
-        out = []
-        for a, b in ((s, v), (s, y), (s, z), (y, r), (y, v), (z, r), (z, v), (y, z)):
-            out += dot(a, b)
-        return out + [norm(y), norm(z), norm(s)]
-
-    def block(k, c, x, zh, r):
-        return w[k, c, 0, x, zh, pl.ds(r, TILE)], w[k, c, 1, x, zh, pl.ds(r, TILE)]
-
-    def over_blocks(body, carry):
-        def at_row(c, x, zh, t, carry):
-            return body(c, x, zh, pl.multiple_of(t * TILE + TILE, TILE), carry)
-
-        tiles = rows // TILE
-
-        def step(i, carry):
-            t, q = lax.rem(i, tiles), i // tiles
-            x, c = lax.rem(q, layers) + 1, q // layers
-            for zh in both:
-                carry = at_row(c, x, zh, t, carry)
-            return carry
-
-        return lax.fori_loop(0, 3 * layers * tiles, step, carry)
-
-    def combine(coefs, basis):
-        total = None
-        for c, b in zip(coefs, basis):
-            if c is None:
-                continue
-            term = cmul(c, b)
-            total = term if total is None else cadd(total, term)
-        return total
-
-    def save(base, values):
-        for i, v in enumerate(values):
-            coef[2 * (base + i)], coef[2 * (base + i) + 1] = v
-
-    def load(base, n):
-        return [get_coef(base + i) for i in range(n)]
-
-    R0, P0, X0, RHO = 0, 5, 10, 14
-    zero_pair = (zero, zero)
-    one_pair = (jnp.ones((TILE, LANES), f32), zero)
-
-    def shift(a):
-        return [None] + list(a)
-
-    def minus(a, b, factor_):
-        n = max(len(a), len(b))
-        out = []
-        for i in range(n):
-            left = a[i] if i < len(a) else None
-            right = b[i] if i < len(b) else None
-            right = None if right is None else cmul(factor_, right)
-            if left is None and right is None:
-                out.append(None)
-            elif right is None:
-                out.append(left)
-            elif left is None:
-                out.append(cneg(right))
-            else:
-                out.append(csub(left, right))
-        return out
-
-    def advance(it):
-        values = reduced(it)
-        if it == 0:
-            r, p, x = [one_pair], [one_pair], []
-            rho, alpha, weight, rho_next = scalars(values, None)
-        else:
-            n = 2 * it + 1
-            r, p, x = load(R0, n), load(P0, n), load(X0, n - 1)
-            rho, alpha, weight, rho_next = scalars(values, get_coef(RHO))
-        v = shift(p)
-        m = minus(r, v, alpha)
-        t = shift(m)
-        x = minus(x, p, cneg(alpha))
-        x = minus(x, m, cneg(weight))
-        r_next = minus(m, t, weight)
-        beta = cmul(cdiv(rho_next, rho), cdiv(alpha, weight))
-        p_next = minus(r_next, minus(p, v, weight), cneg(beta))
-        save(R0, r_next)
-        save(P0, p_next)
-        save(X0, x)
-        save(RHO, [rho_next])
-
-    def gather_products(it):
-        n = 2 * it + 1
-
-        def body(c, x, zh, r_, carry):
-            basis = [block(k, c, x, zh, r_) for k in range(2 * it + 3)]
-            if it == 0:
-                r, v, y, z = basis[0], basis[1], basis[1], basis[2]
-            else:
-                rc, pc = load(R0, n), load(P0, n)
-                r = combine(rc, basis)
-                v, y = combine(pc, basis[1:]), combine(rc, basis[1:])
-                z = combine(pc, basis[2:])
-            if it == ITERS - 1:
-                for i, value in enumerate((r, v, y, z)):
-                    for ri in range(2):
-                        vecs[i, c, ri, x - 1, zh, pl.ds(r_ - TILE, TILE)] = value[ri]
-            return [a + b for a, b in zip(carry, products(basis[0], r, v, y, z))]
-
-        totals = over_blocks(body, [jnp.zeros((TILE, LANES), f32)] * VALUES)
-        reduce_and_send(it, totals)
-
-    pl.semaphore_wait(barrier, 2 * ny + 1)
-    pass_token(0, 1)
-    for copy in loads():
-        copy.wait()
-    for t in range(tiles):
-        start_if(has_low, down(0, t))
+        last = get_coef(P0 + 2)
+        r, p = load(R0, 3), load(P0, 3)
+        update(r, p, load(X0, 2), plus(r, shift(p), cneg(alpha)), alpha, weight, rho, rho_next)
+        return last
+
+    def gather_last(last):
+        alpha, weight, beta = get_coef(ALPHA), get_coef(WEIGHT), get_coef(BETA)
+        both_last = cmul(beta, weight)
+
+        def body(c, x, zh, r_):
+            r, v, y, z, ay, az, aay, aaz = (kept(i, c, x, zh, r_) for i in range(8))
+            source_, top_w = block(0, c, x, zh, r_), block(STEPS, c, x, zh, r_)
+            aaz = cadd(aaz, cmul(last, top_w))
+            m, t, at, aat = (csub(a, cmul(alpha, b)) for a, b in ((r, v), (y, z), (ay, az), (aay, aaz)))
+            r2, y2, ay2 = (csub(a, cmul(weight, b)) for a, b in ((m, t), (t, at), (at, aat)))
+            v2 = cadd(y2, csub(cmul(beta, v), cmul(both_last, z)))
+            z2 = cadd(ay2, csub(cmul(beta, z), cmul(both_last, az)))
+            for i, value in ((R, r2), (V, v2), (Y, y2), (Z, z2)):
+                keep(i, c, x, zh, r_, value)
+            return products(r2, v2, y2, z2, ((source_, v2),))
+
+        reduce_and_send(2, over_blocks(body, 14))
+
+    with jax.named_scope("wait_loads"):
+        for copy in load_source():
+            copy.wait()
     for t in range(tiles):
         upward(0, TILE + t * TILE)
-        start_if(has_high, up(0, t))
-    across(0).start()
-    start_if(sends_corner, corner(0))
-    for c in range(3):
-        for x in range(layers):
-            for zh in both:
-                mat[c, x, zh] = (freq * freq) * eps[c, x, zh]
+    with jax.named_scope("wait_barrier"):
+        pl.semaphore_wait(barrier, 2 * ny + 1)
+    with jax.named_scope("first_sends"):
+        start_if(sends_corner, corner(0))
+        across(0).start()
+
+        @pl.when(iy == 0)
+        def _():
+            for t in reversed(range(tiles)):
+                start_if(has_low, down(0, t))
+                start_if(has_high, up(0, t))
+
+        @pl.when(iy > 0)
+        def _():
+            for t in range(tiles):
+                start_if(has_low, down(0, t))
+                start_if(has_high, up(0, t))
+
+    with jax.named_scope("tokens"):
+        pass_token(0, 1)
+    with jax.named_scope("load_rest"):
+        for copy in load_rest():
+            copy.wait()
+    with jax.named_scope("mat"):
+        for c in range(3):
+            for x in range(layers):
+                for zh in both:
+                    mat[c, x, zh] = (freq * freq) * eps[c, x, zh]
+
+    lower_core, upper_core = iy == 0, iy == ny - 1
 
     def step(k, carry):
-        @pl.when(k < TOKENS - 1)
-        def _():
-            pl.semaphore_wait(token.at[k], 2)
-            pass_token(k + 1, 2 * (k + 1))
+        more = k + 1 < STEPS
+
+        @pl.when(k == 1)
+        def _():
+            with jax.named_scope("gather_early"):
+                gather_early()
 
         @pl.when(k == 2)
         def _():
             pl.semaphore_wait(token.at[TOKENS - 1], 2)
-            gather_products(0)
+            with jax.named_scope("gather_0"):
+                gather_first()
 
         @pl.when(k == 4)
         def _():
-            advance(0)
-            gather_products(1)
-
-        across(k).wait_recv()
-        for x in range(1, layers):
-            magnetic_layer(k, x)
-        for x in range(2, layers):
-            electric_layer(k, x)
-        more = k + 1 < STEPS
-        lower_core, upper_core = iy == 0, iy == ny - 1
-        for t in range(tiles):
-            r = TILE + t * TILE
-            wait_recv_if(has_low, up(k, t))
-            if t == tiles - 1:
-                wait_recv_if(lower_core & gets_corner, corner(k))
-            magnetic_below(k, r)
-            electric(k, 1, r)
+            with jax.named_scope("advance_0"):
+                advance_first()
+            with jax.named_scope("gather_1"):
+                gather_middle()
+
+        @pl.when(k == 5)
+        def _():
+            with jax.named_scope("look_ahead"):
+                look_ahead()
+
+        with jax.named_scope("inner"):
+            for x in range(1, layers):
+                for r in range(TILE, top - TILE, TILE):
+                    magnetic(k, x, r)
+        with jax.named_scope("wait_across"):
+            across(k).wait_recv()
+        with jax.named_scope("interior"):
+            for x in range(1, layers):
+                magnetic(k, x, 0, True)
+                magnetic(k, x, top - TILE)
+            for x in range(2, layers):
+                electric_layer(k, x)
+
+        def low(t, first=None):
+            wait_recv_if(has_low, up(k, t), f"wait_up_{t}")
+            magnetic_below(k, TILE + t * TILE)
+            electric(k, 1, TILE + t * TILE)
+            if first is not None:
+                start_if(more & sends_corner, first)
             start_if(more & has_low, down(k + 1, t))
-            wait_recv_if(has_high, down(k, t))
-            if t == 0:
-                wait_recv_if(upper_core & gets_corner, corner(k))
-                magnetic(k, layers, 0, True)
-            magnetic(k, layers, r)
-            electric(k, layers, r)
-            if t == 0:
-                start_if(more & upper_core & sends_corner, corner(k + 1))
-                start_if(more & upper_core, across(k + 1))
-            else:
-                @pl.when(more)
-                def _():
-                    upward(k + 1, r - TILE)
-                start_if(more & has_high, up(k + 1, t - 1))
-
-        @pl.when(more)
-        def _():
-            upward(k + 1, top - TILE)
-        start_if(more & has_high, up(k + 1, tiles - 1))
-        start_if(more & lower_core & sends_corner, corner(k + 1))
-        start_if(more & lower_core, across(k + 1))
+
+        def high_magnetic(t):
+            wait_recv_if(has_high, down(k, t), f"wait_down_{t}")
+            magnetic(k, layers, TILE + t * TILE)
+
+        def high_electric(t):
+            electric(k, layers, TILE + t * TILE)
+
+        def send_up(t):
+            @pl.when(more)
+            def _():
+                upward(k + 1, TILE + t * TILE)
+            start_if(more & has_high, up(k + 1, t))
+
+        last = tiles - 1
+
+        @pl.when(k == 0)
+        def _():
+            pl.semaphore_wait(token.at[0], 2)
+            pass_token(1, 2)
+
+        @pl.when(lower_core)
+        def _():
+            high_magnetic(last)
+            high_magnetic(last - 1)
+            high_electric(last)
+            send_up(last)
+            wait_recv_if(gets_corner, corner(k), "wait_corner_l")
+            low(last, corner(k + 1))
+            start_if(more, across(k + 1))
+            for t in range(last - 1, 0, -1):
+                high_magnetic(t - 1)
+                high_electric(t)
+                send_up(t)
+                if t == 1:
+                    magnetic(k, layers, 0, True)
+                    high_electric(0)
+                    send_up(0)
+                low(t)
+            low(0)
+
+        @pl.when(upper_core)
+        def _():
+            wait_recv_if(gets_corner, corner(k), "wait_corner_u")
+            magnetic(k, layers, 0, True)
+            high_magnetic(0)
+            high_electric(0)
+            start_if(more & sends_corner, corner(k + 1))
+            high_magnetic(1)
+            high_electric(1)
+            send_up(0)
+            low(0)
+            start_if(more, across(k + 1))
+            for t in range(2, tiles):
+                high_magnetic(t)
+                high_electric(t)
+                send_up(t - 1)
+                if t == last:
+                    send_up(t)
+                low(t - 1)
+            low(last)
+
+        @pl.when(k == 0)
+        def _():
+            pl.semaphore_wait(token.at[1], 2)
+            pass_token(2, 4)
+
         return carry
 
     lax.fori_loop(0, STEPS, step, 0)
-    advance(1)
-    gather_products(2)
+    with jax.named_scope("advance_1"):
+        last = advance_middle()
+    with jax.named_scope("gather_2"):
+        gather_last(last)
 
     n = 2 * ITERS - 1
-
-    def partial(c, x, zh, r_, carry):
+    x_coef, p_coef = load(X0, n - 1), load(P0, n)
+
+    def partial(c, x, zh, r_):
         basis = [block(k, c, x, zh, r_) for k in range(n)]
-        xs, ps = combine(load(X0, n - 1), basis), combine(load(P0, n), basis)
-        for ri in range(2):
-            vecs[4, c, ri, x - 1, zh, pl.ds(r_ - TILE, TILE)] = xs[ri]
-            vecs[5, c, ri, x - 1, zh, pl.ds(r_ - TILE, TILE)] = ps[ri]
-        return carry
-
-    over_blocks(partial, 0)
+        keep(XS, c, x, zh, r_, combine(x_coef, basis))
+        keep(PS, c, x, zh, r_, combine(p_coef, basis))
+
+    with jax.named_scope("partial"):
+        over_blocks(partial, 0)
 
     def finish_sends(k, carry):
         for t in range(tiles):
@@ -611,25 +742,21 @@
     for rnd in range(ITERS - 1):
         bulk(rnd).wait_send()
 
-    values = reduced(ITERS - 1)
-    rho, alpha, weight, _ = scalars(values, get_coef(RHO))
-    both_factors = cmul(alpha, weight)
-
-    for c in range(3):
-        def write(i, carry):
-            t, x = lax.rem(i, rows // TILE), i // (rows // TILE)
-            r_ = pl.multiple_of(t * TILE, TILE)
-            for zh in both:
-                r, v, y, z, xs, ps = (
-                    tuple(vecs[q, c, ri, x, zh, pl.ds(r_, TILE)] for ri in range(2)) for q in range(6))
-                new_x = cadd(xs, cadd(cmul(alpha, ps), csub(cmul(weight, r), cmul(both_factors, v))))
-                new_r = cadd(csub(csub(r, cmul(alpha, v)), cmul(weight, y)), cmul(both_factors, z))
-                for ri in range(2):
-                    sol[0, ORDER[c], ri, x, pl.ds(r_, TILE), pl.ds(zh * LANES, LANES)] = new_x[ri]
-                    res[0, ORDER[c], ri, x, pl.ds(r_, TILE), pl.ds(zh * LANES, LANES)] = new_r[ri]
-            return carry
-
-        lax.fori_loop(0, layers * (rows // TILE), write, 0)
+    with jax.named_scope("reduced_2"):
+        (_, alpha, weight), _ = read_products(reduced(2, 14), 1)
+    both_steps = cmul(alpha, weight)
+
+    with jax.named_scope("final"):
+        def write(c, x, zh, r_):
+            r, v, y, z, xs, ps = (kept(i, c, x, zh, r_) for i in (R, V, Y, Z, XS, PS))
+            new_x = cadd(cadd(xs, cmul(alpha, ps)), csub(cmul(weight, r), cmul(both_steps, v)))
+            new_r = cadd(csub(r, cmul(alpha, v)), csub(cmul(both_steps, z), cmul(weight, y)))
+            at = jnp.where(c == 0, 0, 3 - c)
+            for ri in range(2):
+                for ref, value in ((sol, new_x), (res, new_r)):
+                    ref[0, at, ri, x - 1, pl.ds(r_ - TILE, TILE), pl.ds(zh * LANES, LANES)] = value[ri]
+
+        over_blocks(write, 0)
     bulk(ITERS - 1).wait_send()
 
 
@@ -664,8 +791,8 @@
                 vmem(3, layers, halves, rows, LANES),
                 vmem(ITERS, nx * ny, 1, LANES),
                 vmem(ITERS, 1, LANES),
-                vmem(6, 3, 2, layers, halves, rows, LANES),
-                vmem(30, TILE, LANES),
+                vmem(10, 3, 2, layers, halves, rows, LANES),
+                vmem(2 * 18, TILE, LANES),
                 pltpu.SemaphoreType.DMA((6 * halves,)),
                 pltpu.SemaphoreType.DMA((STEPS, 2 * (rows // TILE) + 2)),
                 pltpu.SemaphoreType.DMA((STEPS, 2 * (rows // TILE) + 2)),
@@ -676,7 +803,7 @@
             compiler_params=pltpu.CompilerParams(
                 collective_id=0, has_side_effects=True, vmem_limit_bytes=48 * 1024 * 1024
             ),
-        )(source, permittivity, frequency)
+        )(*(pltpu.with_memory_space_constraint(a, pltpu.HBM) for a in (source, permittivity)), frequency)
 
     placed = P("groups", None, None, "gx", "gy", None)
     return jax.shard_map(

time: 64 us -> 54.4 us (0.85)
  Pallas kernels: 58.7 us -> 51.3 us
  local copies, waits for them, and re-layouts: 3.88 us -> 1.76 us
    pallas_call x1, Pallas kernels: 58.7 us -> 51.3 us  [body(): pl.pallas_call(functools.partial(kernel, nx, ny), out_shape=(jax.ShapeDty...]
    unnamed x6 -> x2, local copies, waits for them, and re-layouts: 3.88 us -> 1.76 us
where the time goes in v3:
time: 54.4 us; the launch traced here: 54.3 us
  Pallas kernels  51.3 us (94%)
  local copies, waits for them, and re-layouts  1.76 us (3%)
  between operations  1.28 us (2%)
    pallas_call x1, Pallas kernels, body(): pl.pallas_call(functools.partial(kernel, nx, ny), out_shape=(jax.ShapeDty...  51.3 us
    unnamed x2, local copies, waits for them, and re-layouts  1.76 us

profile of v3, /device:TPU:69, one launch (start us, length us, event | category | flops | bytes accessed | tf_op | source)
XLA Modules:
  0.0 54.3 jit_solution(2667240463188612847)
XLA Ops:
  1.3 51.3 %shard_map.50 = (f32[1,3,2,4,32,256]{5,4,3,2,1,0:T(8,128)S(1)}, f32[1,3,2,4,32,256]{5,4,3,2,1,0:T(8,128)S(1)}) custom-call(f32[1,3,2,4,32,256]{5,4,3,2,1,0:T(8,128)} %source.1, f32[3,4,32,256]{3,2,1,0:T(8,128)} %permittivity.1, f32[1]{0:T(128)S(6)} %copy.7.frequency), custom_call_target="tpu_custom_call" | custom-call | tf_op jit(solution)/shard_map/pallas_call | solution.py:770
  52.5 0.9 %copy.8 = f32[1,3,2,4,32,256]{5,4,3,2,1,0:T(8,128)} copy(f32[1,3,2,4,32,256]{5,4,3,2,1,0:T(8,128)S(1)} %get-tuple-element.4) | data formatting | bytes 1572864
  53.4 0.9 %copy.9 = f32[1,3,2,4,32,256]{5,4,3,2,1,0:T(8,128)} copy(f32[1,3,2,4,32,256]{5,4,3,2,1,0:T(8,128)S(1)} %get-tuple-element.5) | data formatting | bytes 1572864

commit v4 on v3

--- a/solution.py
+++ b/solution.py
@@ -12,6 +12,8 @@
 STRENGTH = 2.0
 STEPS = 2 * ITERS
 PER = 4
+R, V, Y, Z, XS, PS, AY, AZ, AAY, AAZ = range(10)
+HANDED = 6
 CX, CZ, CY = 0, 1, 2
 ORDER = (0, 2, 1)
 LANES = 128
@@ -74,7 +76,7 @@
 
 
 def kernel(
-    nx, ny, source, permittivity, frequency, sol, res,
+    nx, ny, source, permittivity, frequency, handed, scalars,
     w, h, gsend, grecv, mat, fx, bx, fy, by, fz, bz, eps, red, row, vecs, coef,
     load_sem, x_send, x_recv, red_send, red_recv, token,
 ):
@@ -492,35 +494,45 @@
         return steps_of(get_coef(RHO), sv, yr, yv, zr, zv, yz, yy, zz), pairs[6:]
 
     def keep(i, c, x, zh, r_, value):
+        ref, i = (handed, i) if i < HANDED else (vecs, i - HANDED)
         for ri in range(2):
-            vecs[i, c, ri, x - 1, zh, pl.ds(r_ - TILE, TILE)] = value[ri]
+            ref[i, c, ri, x - 1, zh, pl.ds(r_ - TILE, TILE)] = value[ri]
 
     def kept(i, c, x, zh, r_):
-        return tuple(vecs[i, c, ri, x - 1, zh, pl.ds(r_ - TILE, TILE)] for ri in range(2))
-
-    R, V, Y, Z, AY, AZ, AAY, AAZ, XS, PS = range(10)
+        ref, i = (handed, i) if i < HANDED else (vecs, i - HANDED)
+        return tuple(ref[i, c, ri, x - 1, zh, pl.ds(r_ - TILE, TILE)] for ri in range(2))
+
+
+    def middle_scalars():
+        weight, beta = get_coef(WEIGHT), get_coef(BETA)
+        return get_coef(R0 + 1), get_coef(R0 + 2), beta, cneg(cmul(beta, weight))
 
     def gather_middle():
-        rc, pc = load(R0, 3), load(P0, 3)
+        c1, c2, beta, back = middle_scalars()
 
         def body(c, x, zh, r_):
-            basis = [block(k, c, x, zh, r_) for k in range(5)]
-            r, v, y, z = combine(rc, basis), combine(pc, basis[1:]), combine(rc, basis[1:]), combine(pc, basis[2:])
-            for i, value in ((R, r), (V, v), (Y, y), (Z, z)):
+            w0, w1, w2, w3, w4 = (block(k, c, x, zh, r_) for k in range(5))
+            r = cadd(w0, combine((c1, c2), (w1, w2)))
+            y = cadd(w1, combine((c1, c2), (w2, w3)))
+            ay = cadd(w2, combine((c1, c2), (w3, w4)))
+            v = cadd(y, combine((beta, back), (w1, w2)))
+            z = cadd(ay, combine((beta, back), (w2, w3)))
+            for i, value in ((R, r), (V, v), (Y, y), (Z, z), (AY, ay)):
                 keep(i, c, x, zh, r_, value)
-            return products(r, v, y, z, tuple((basis[0], b) for b in (v, y, z)))
+            return products(r, v, y, z, tuple((w0, b) for b in (v, y, z)))
 
         reduce_and_send(1, over_blocks(body, 18))
 
     def look_ahead():
-        rc, pc = load(R0, 3), load(P0, 3)
+        c1, c2, beta, back = middle_scalars()
+        c1_back = cadd(c1, back)
 
         def body(c, x, zh, r_):
-            basis = [block(k, c, x, zh, r_) for k in range(2, 6)]
-            for i, value in (
-                (AY, combine(rc, basis)), (AZ, combine(pc, basis[1:])),
-                (AAY, combine(rc, basis[1:])), (AAZ, combine(pc, basis[2:])),
-            ):
+            w3, w4, w5 = (block(k, c, x, zh, r_) for k in range(3, 6))
+            aay = cadd(w3, combine((c1, c2), (w4, w5)))
+            az = cadd(aay, combine((beta, back), (w3, w4)))
+            aaz = cadd(w4, combine((beta, c1_back), (w4, w5)))
+            for i, value in ((AZ, az), (AAY, aay), (AAZ, aaz)):
                 keep(i, c, x, zh, r_, value)
 
         over_blocks(body, 0)
@@ -529,7 +541,7 @@
         values = reduced(1, 18)
         (rho, alpha, weight), (sy, sz) = read_products(values, 3)
         rho_next = cneg(cmul(weight, csub(sy, cmul(alpha, sz))))
-        last = get_coef(P0 + 2)
+        last = get_coef(R0 + 2)
         r, p = load(R0, 3), load(P0, 3)
         update(r, p, load(X0, 2), plus(r, shift(p), cneg(alpha)), alpha, weight, rho, rho_next)
         return last
@@ -539,7 +551,7 @@
         both_last = cmul(beta, weight)
 
         def body(c, x, zh, r_):
-            r, v, y, z, ay, az, aay, aaz = (kept(i, c, x, zh, r_) for i in range(8))
+            r, v, y, z, ay, az, aay, aaz = (kept(i, c, x, zh, r_) for i in (R, V, Y, Z, AY, AZ, AAY, AAZ))
             source_, top_w = block(0, c, x, zh, r_), block(STEPS, c, x, zh, r_)
             aaz = cadd(aaz, cmul(last, top_w))
             m, t, at, aat = (csub(a, cmul(alpha, b)) for a, b in ((r, v), (y, z), (ay, az), (aay, aaz)))
@@ -627,26 +639,44 @@
             for x in range(2, layers):
                 electric_layer(k, x)
 
-        def low(t, first=None):
-            wait_recv_if(has_low, up(k, t), f"wait_up_{t}")
+        def wait_down(*ts):
+            with jax.named_scope("wait_down"):
+                @pl.when(has_high)
+                def _():
+                    for t in ts:
+                        down(k, t).wait_recv()
+
+        def wait_up(*ts):
+            with jax.named_scope("wait_up"):
+                @pl.when(has_low)
+                def _():
+                    for t in ts:
+                        up(k, t).wait_recv()
+
+        def send_down(*ts):
+            @pl.when(more & has_low)
+            def _():
+                for t in ts:
+                    down(k + 1, t).start()
+
+        def send_up(*ts):
+            @pl.when(more & has_high)
+            def _():
+                for t in ts:
+                    up(k + 1, t).start()
+
+        def low(t):
             magnetic_below(k, TILE + t * TILE)
             electric(k, 1, TILE + t * TILE)
-            if first is not None:
-                start_if(more & sends_corner, first)
-            start_if(more & has_low, down(k + 1, t))
 
         def high_magnetic(t):
-            wait_recv_if(has_high, down(k, t), f"wait_down_{t}")
             magnetic(k, layers, TILE + t * TILE)
 
         def high_electric(t):
             electric(k, layers, TILE + t * TILE)
 
-        def send_up(t):
-            @pl.when(more)
-            def _():
-                upward(k + 1, TILE + t * TILE)
-            start_if(more & has_high, up(k + 1, t))
+        def form_up(t):
+            upward(k + 1, TILE + t * TILE)
 
         last = tiles - 1
 
@@ -657,44 +687,82 @@
 
         @pl.when(lower_core)
         def _():
+            wait_down(last)
             high_magnetic(last)
+            wait_down(last - 1)
             high_magnetic(last - 1)
             high_electric(last)
+            form_up(last)
             send_up(last)
             wait_recv_if(gets_corner, corner(k), "wait_corner_l")
-            low(last, corner(k + 1))
+            wait_up(last)
+            low(last)
+            start_if(more & sends_corner, corner(k + 1))
+            send_down(last)
             start_if(more, across(k + 1))
-            for t in range(last - 1, 0, -1):
+            for t in range(last - 1, 1, -1):
+                wait_down(t - 1)
                 high_magnetic(t - 1)
                 high_electric(t)
+                form_up(t)
                 send_up(t)
-                if t == 1:
-                    magnetic(k, layers, 0, True)
-                    high_electric(0)
-                    send_up(0)
+                wait_up(t)
                 low(t)
+                send_down(t)
+            wait_down(0)
+            high_magnetic(0)
+            high_electric(1)
+            form_up(1)
+            send_up(1)
+            magnetic(k, layers, 0, True)
+            high_electric(0)
+            form_up(0)
+            send_up(0)
+            wait_up(1)
+            low(1)
+            send_down(1)
+            wait_up(0)
             low(0)
+            send_down(0)
 
         @pl.when(upper_core)
         def _():
             wait_recv_if(gets_corner, corner(k), "wait_corner_u")
+            wait_down(0)
             magnetic(k, layers, 0, True)
             high_magnetic(0)
             high_electric(0)
             start_if(more & sends_corner, corner(k + 1))
+            wait_down(1)
             high_magnetic(1)
             high_electric(1)
+            form_up(0)
             send_up(0)
+            wait_up(0)
             low(0)
+            send_down(0)
             start_if(more, across(k + 1))
-            for t in range(2, tiles):
+            for t in range(2, last):
+                wait_down(t)
                 high_magnetic(t)
                 high_electric(t)
+                form_up(t - 1)
                 send_up(t - 1)
-                if t == last:
-                    send_up(t)
+                wait_up(t - 1)
                 low(t - 1)
+                send_down(t - 1)
+            wait_down(last)
+            high_magnetic(last)
+            high_electric(last)
+            form_up(last - 1)
+            form_up(last)
+            send_up(last - 1, last)
+            wait_up(last - 1)
+            low(last - 1)
+            send_down(last - 1)
+            wait_up(last)
             low(last)
+            send_down(last)
 
         @pl.when(k == 0)
         def _():
@@ -744,20 +812,44 @@
 
     with jax.named_scope("reduced_2"):
         (_, alpha, weight), _ = read_products(reduced(2, 14), 1)
+    for i, value in enumerate(alpha + weight):
+        scalars[i] = value
+    bulk(ITERS - 1).wait_send()
+
+
+def finish(handed, scalars, sol_out, res_out, sol, res, sem):
+    layers, halves, rows = handed.shape[3:6]
+    alpha, weight = (scalars[0], scalars[1]), (scalars[2], scalars[3])
     both_steps = cmul(alpha, weight)
 
-    with jax.named_scope("final"):
-        def write(c, x, zh, r_):
-            r, v, y, z, xs, ps = (kept(i, c, x, zh, r_) for i in (R, V, Y, Z, XS, PS))
-            new_x = cadd(cadd(xs, cmul(alpha, ps)), csub(cmul(weight, r), cmul(both_steps, v)))
-            new_r = cadd(csub(r, cmul(alpha, v)), csub(cmul(both_steps, z), cmul(weight, y)))
-            at = jnp.where(c == 0, 0, 3 - c)
-            for ri in range(2):
-                for ref, value in ((sol, new_x), (res, new_r)):
-                    ref[0, at, ri, x - 1, pl.ds(r_ - TILE, TILE), pl.ds(zh * LANES, LANES)] = value[ri]
-
-        over_blocks(write, 0)
-    bulk(ITERS - 1).wait_send()
+    def copies(c, x):
+        return [
+            pltpu.make_async_copy(ref.at[0, c, :, x], out.at[0, c, :, x], sem.at[i, c, x])
+            for i, (ref, out) in enumerate(((sol, sol_out), (res, res_out)))
+        ]
+
+    def layer(i, carry):
+        c, x = i // layers, lax.rem(i, layers)
+        at = jnp.where(c == 0, 0, 3 - c)
+        for t in range(rows // TILE):
+            for zh in range(halves):
+                r, v, y, z, xs, ps = (
+                    tuple(handed[q, c, ri, x, zh, pl.ds(t * TILE, TILE)] for ri in range(2))
+                    for q in (R, V, Y, Z, XS, PS))
+                new_x = cadd(cadd(xs, cmul(alpha, ps)), csub(cmul(weight, r), cmul(both_steps, v)))
+                new_r = cadd(csub(r, cmul(alpha, v)), csub(cmul(both_steps, z), cmul(weight, y)))
+                for ri in range(2):
+                    for ref, value in ((sol, new_x), (res, new_r)):
+                        ref[0, at, ri, x, pl.ds(t * TILE, TILE), pl.ds(zh * LANES, LANES)] = value[ri]
+        for copy in copies(at, x):
+            copy.start()
+        return carry
+
+    lax.fori_loop(0, 3 * layers, layer, 0)
+    for c in range(3):
+        for x in range(layers):
+            for copy in copies(c, x):
+                copy.wait()
 
 
 def solution(mesh):
@@ -767,9 +859,12 @@
         layers, rows, depth = source.shape[3:]
         halves = depth // LANES
         vmem = lambda *shape: pltpu.VMEM(shape, f32)
-        return pl.pallas_call(
+        handed, scalars = pl.pallas_call(
             functools.partial(kernel, nx, ny),
-            out_shape=(jax.ShapeDtypeStruct(source.shape, f32),) * 2,
+            out_shape=(
+                jax.ShapeDtypeStruct((HANDED, 3, 2, layers, halves, rows, LANES), f32),
+                jax.ShapeDtypeStruct((4, TILE, LANES), f32),
+            ),
             in_specs=[
                 pl.BlockSpec(memory_space=pltpu.HBM),
                 pl.BlockSpec(memory_space=pltpu.HBM),
@@ -779,7 +874,7 @@
             scratch_shapes=[
                 vmem(STEPS + 1, 3, 2, layers + 2, halves, rows + 2 * TILE, LANES),
                 vmem(3, 2, layers + 1, halves, rows + TILE, LANES),
-                vmem(STEPS, 2, 2, halves, rows, LANES),
+                vmem(STEPS + 1, 2, 2, halves, rows, LANES),
                 vmem(STEPS, 2, 2, halves, rows, LANES),
                 vmem(3, layers, halves, rows, LANES),
                 vmem(layers + 1, 2, 1, LANES),
@@ -791,7 +886,7 @@
                 vmem(3, layers, halves, rows, LANES),
                 vmem(ITERS, nx * ny, 1, LANES),
                 vmem(ITERS, 1, LANES),
-                vmem(10, 3, 2, layers, halves, rows, LANES),
+                vmem(4, 3, 2, layers, halves, rows, LANES),
                 vmem(2 * 18, TILE, LANES),
                 pltpu.SemaphoreType.DMA((6 * halves,)),
                 pltpu.SemaphoreType.DMA((STEPS, 2 * (rows // TILE) + 2)),
@@ -804,6 +899,18 @@
                 collective_id=0, has_side_effects=True, vmem_limit_bytes=48 * 1024 * 1024
             ),
         )(*(pltpu.with_memory_space_constraint(a, pltpu.HBM) for a in (source, permittivity)), frequency)
+        return pl.pallas_call(
+            finish,
+            out_shape=(jax.ShapeDtypeStruct(source.shape, f32),) * 2,
+            in_specs=[pl.BlockSpec(memory_space=pltpu.VMEM)] * 2,
+            out_specs=(pl.BlockSpec(memory_space=pltpu.HBM),) * 2,
+            scratch_shapes=[
+                vmem(*source.shape),
+                vmem(*source.shape),
+                pltpu.SemaphoreType.DMA((2, 3, layers)),
+            ],
+            compiler_params=pltpu.CompilerParams(vmem_limit_bytes=8 * 1024 * 1024),
+        )(handed, scalars)
 
     placed = P("groups", None, None, "gx", "gy", None)
     return jax.shard_map(

time: 54.4 us -> 53.9 us (level)
  local copies, waits for them, and re-layouts: 1.76 us -> 0 us
  Pallas kernels: 51.3 us -> 52.5 us
    unnamed x2 -> x0, local copies, waits for them, and re-layouts: 1.76 us -> none
    pallas_call x0 -> x1, Pallas kernels: none -> 1.64 us  [body(): pl.pallas_call(finish, out_shape=(jax.ShapeDtypeStruct(source.shape, f32)...]
where the time goes in v4:
time: 53.9 us; the launch traced here: 53.8 us
  Pallas kernels  52.5 us (97%)
  between operations  1.28 us (2%)
    pallas_call x1, Pallas kernels, body(): pl.pallas_call(functools.partial(kernel, nx, ny), out_shape=(jax.ShapeDty...  50.8 us
    pallas_call x1, Pallas kernels, body(): pl.pallas_call(finish, out_shape=(jax.ShapeDtypeStruct(source.shape, f32)...  1.64 us

profile of v4, /device:TPU:69, one launch (start us, length us, event | category | flops | bytes accessed | tf_op | source)
XLA Modules:
  0.0 53.8 jit_solution(9821003293455552020)
XLA Ops:
  1.3 50.8 %shard_map.50 = (f32[6,3,2,4,2,32,128]{6,5,4,3,2,1,0:T(8,128)S(1)}, f32[4,8,128]{2,1,0:T(8,128)S(1)}) custom-call(f32[1,3,2,4,32,256]{5,4,3,2,1,0:T(8,128)} %source.1, f32[3,4,32,256]{3,2,1,0:T(8,128)} %permittivity.1, f32[1]{0:T(128)S(6)} %copy.5.frequency), custom_call_target="tpu_custom_call" | custom-call | tf_op jit(solution)/shard_map/pallas_call | solution.py:862
  52.1 1.6 %shard_map.51 = (f32[1,3,2,4,32,256]{5,4,3,2,1,0:T(8,128)}, f32[1,3,2,4,32,256]{5,4,3,2,1,0:T(8,128)}) custom-call(f32[6,3,2,4,2,32,128]{6,5,4,3,2,1,0:T(8,128)S(1)} %get-tuple-element.4.handed, f32[4,8,128]{2,1,0:T(8,128)S(1)} %get-tuple-element.5.scalars), custom_call_target="tpu_custom_call" | custom-call | tf_op jit(solution)/shard_map/pallas_call | solution.py:902

commit v5 on v4

--- a/solution.py
+++ b/solution.py
@@ -96,11 +96,6 @@
     def ring(distance):
         return lax.rem(ix + distance, nx), lax.rem(ix + nx - distance, nx)
 
-    for gx in ring(1):
-        for gy in range(ny):
-            signal(barrier, gx, gy)
-    signal(barrier, ix, 1 - iy)
-
     def pass_token(index, distance):
         for gx in ring(distance):
             signal(token.at[index], gx, iy)
@@ -122,7 +117,15 @@
             for c in range(3) for zh in range(halves)
         ]
 
-    for copy in load_source() + load_rest():
+    for copy in load_source():
+        copy.start()
+
+    for gx in ring(1):
+        for gy in range(ny):
+            signal(barrier, gx, gy)
+    signal(barrier, ix, 1 - iy)
+
+    for copy in load_rest():
         copy.start()
 
     zero = jnp.zeros((TILE, LANES), f32)
@@ -687,6 +690,11 @@
 
         @pl.when(lower_core)
         def _():
+            wait_recv_if(gets_corner, corner(k), "wait_corner_l")
+            wait_up(last)
+            low(last)
+            start_if(more & sends_corner, corner(k + 1))
+            send_down(last)
             wait_down(last)
             high_magnetic(last)
             wait_down(last - 1)
@@ -694,21 +702,19 @@
             high_electric(last)
             form_up(last)
             send_up(last)
-            wait_recv_if(gets_corner, corner(k), "wait_corner_l")
-            wait_up(last)
-            low(last)
-            start_if(more & sends_corner, corner(k + 1))
-            send_down(last)
             start_if(more, across(k + 1))
             for t in range(last - 1, 1, -1):
+                wait_up(t)
+                low(t)
+                send_down(t)
                 wait_down(t - 1)
                 high_magnetic(t - 1)
                 high_electric(t)
                 form_up(t)
                 send_up(t)
-                wait_up(t)
-                low(t)
-                send_down(t)
+            wait_up(1)
+            low(1)
+            send_down(1)
             wait_down(0)
             high_magnetic(0)
             high_electric(1)
@@ -718,9 +724,6 @@
             high_electric(0)
             form_up(0)
             send_up(0)
-            wait_up(1)
-            low(1)
-            send_down(1)
             wait_up(0)
             low(0)
             send_down(0)

time: 53.9 us -> 53.3 us (0.989)
  Pallas kernels: 52.5 us -> 51.9 us
    pallas_call x1, Pallas kernels: 50.8 us -> 50.2 us  [body(): pl.pallas_call(functools.partial(kernel, nx, ny), out_shape=(jax.ShapeDty...]
where the time goes in v5:
time: 53.3 us; the launch traced here: 53.2 us
  Pallas kernels  51.9 us (97%)
  between operations  1.28 us (2%)
    pallas_call x1, Pallas kernels, body(): pl.pallas_call(functools.partial(kernel, nx, ny), out_shape=(jax.ShapeDty...  50.2 us
    pallas_call x1, Pallas kernels, body(): pl.pallas_call(finish, out_shape=(jax.ShapeDtypeStruct(source.shape, f32)...  1.64 us

profile of v5, /device:TPU:69, one launch (start us, length us, event | category | flops | bytes accessed | tf_op | source)
XLA Modules:
  0.0 53.2 jit_solution(3562880979096753280)
XLA Ops:
  1.3 50.2 %shard_map.50 = (f32[6,3,2,4,2,32,128]{6,5,4,3,2,1,0:T(8,128)S(1)}, f32[4,8,128]{2,1,0:T(8,128)S(1)}) custom-call(f32[1,3,2,4,32,256]{5,4,3,2,1,0:T(8,128)} %source.1, f32[3,4,32,256]{3,2,1,0:T(8,128)} %permittivity.1, f32[1]{0:T(128)S(6)} %copy.5.frequency), custom_call_target="tpu_custom_call" | custom-call | tf_op jit(solution)/shard_map/pallas_call | solution.py:865
  51.5 1.6 %shard_map.51 = (f32[1,3,2,4,32,256]{5,4,3,2,1,0:T(8,128)}, f32[1,3,2,4,32,256]{5,4,3,2,1,0:T(8,128)}) custom-call(f32[6,3,2,4,2,32,128]{6,5,4,3,2,1,0:T(8,128)S(1)} %get-tuple-element.4.handed, f32[4,8,128]{2,1,0:T(8,128)S(1)} %get-tuple-element.5.scalars), custom_call_target="tpu_custom_call" | custom-call | tf_op jit(solution)/shard_map/pallas_call | solution.py:905

commit v6 on v5

--- a/solution.py
+++ b/solution.py
@@ -11,7 +11,7 @@
 ITERS = 3
 STRENGTH = 2.0
 STEPS = 2 * ITERS
-PER = 4
+PER = 2
 R, V, Y, Z, XS, PS, AY, AZ, AAY, AAZ = range(10)
 HANDED = 6
 CX, CZ, CY = 0, 1, 2
@@ -399,20 +399,17 @@
         return w[k, c, 0, x, zh, pl.ds(r, TILE)], w[k, c, 1, x, zh, pl.ds(r, TILE)]
 
     def over_blocks(body, n):
-        per = PER
-
         def step(i, carry):
-            q = i // (tiles // per)
-            t = lax.rem(i, tiles // per) * per
-            x, c = lax.rem(q, layers) + 1, q // layers
-            for u in range(per):
-                for zh in both:
-                    out = body(c, x, zh, pl.multiple_of((t + u) * TILE + TILE, TILE))
-                    if n:
-                        carry = [a + b for a, b in zip(carry, out)]
+            c, x = i // (layers // PER), lax.rem(i, layers // PER) * PER + 1
+            for u in range(PER):
+                for t in range(tiles):
+                    for zh in both:
+                        out = body(c, x + u, zh, TILE + t * TILE)
+                        if n:
+                            carry = [a + b for a, b in zip(carry, out)]
             return carry
 
-        return lax.fori_loop(0, 3 * layers * tiles // per, step, [jnp.zeros((TILE, LANES), f32)] * n)
+        return lax.fori_loop(0, 3 * layers // PER, step, [jnp.zeros((TILE, LANES), f32)] * n)
 
     def combine(coefs, basis):
         total = None
@@ -823,7 +820,6 @@
 def finish(handed, scalars, sol_out, res_out, sol, res, sem):
     layers, halves, rows = handed.shape[3:6]
     alpha, weight = (scalars[0], scalars[1]), (scalars[2], scalars[3])
-    both_steps = cmul(alpha, weight)
 
     def copies(c, x):
         return [
@@ -839,8 +835,9 @@
                 r, v, y, z, xs, ps = (
                     tuple(handed[q, c, ri, x, zh, pl.ds(t * TILE, TILE)] for ri in range(2))
                     for q in (R, V, Y, Z, XS, PS))
-                new_x = cadd(cadd(xs, cmul(alpha, ps)), csub(cmul(weight, r), cmul(both_steps, v)))
-                new_r = cadd(csub(r, cmul(alpha, v)), csub(cmul(both_steps, z), cmul(weight, y)))
+                m, t_ = csub(r, cmul(alpha, v)), csub(y, cmul(alpha, z))
+                new_x = cadd(cadd(xs, cmul(alpha, ps)), cmul(weight, m))
+                new_r = csub(m, cmul(weight, t_))
                 for ri in range(2):
                     for ref, value in ((sol, new_x), (res, new_r)):
                         ref[0, at, ri, x, pl.ds(t * TILE, TILE), pl.ds(zh * LANES, LANES)] = value[ri]

time: 53.3 us -> 53 us (level)
  no operation moved by 1% of the time
where the time goes in v6:
time: 53 us; the launch traced here: 52.9 us
  Pallas kernels  51.6 us (97%)
  between operations  1.28 us (2%)
    pallas_call x1, Pallas kernels, body(): pl.pallas_call(functools.partial(kernel, nx, ny), out_shape=(jax.ShapeDty...  50.1 us
    pallas_call x1, Pallas kernels, body(): pl.pallas_call(finish, out_shape=(jax.ShapeDtypeStruct(source.shape, f32)...  1.56 us

profile of v6, /device:TPU:69, one launch (start us, length us, event | category | flops | bytes accessed | tf_op | source)
XLA Modules:
  0.0 52.9 jit_solution(7387297038795249979)
XLA Ops:
  1.3 50.1 %shard_map.50 = (f32[6,3,2,4,2,32,128]{6,5,4,3,2,1,0:T(8,128)S(1)}, f32[4,8,128]{2,1,0:T(8,128)S(1)}) custom-call(f32[1,3,2,4,32,256]{5,4,3,2,1,0:T(8,128)} %source.1, f32[3,4,32,256]{3,2,1,0:T(8,128)} %permittivity.1, f32[1]{0:T(128)S(6)} %copy.5.frequency), custom_call_target="tpu_custom_call" | custom-call | tf_op jit(solution)/shard_map/pallas_call | solution.py:862
  51.3 1.6 %shard_map.51 = (f32[1,3,2,4,32,256]{5,4,3,2,1,0:T(8,128)}, f32[1,3,2,4,32,256]{5,4,3,2,1,0:T(8,128)}) custom-call(f32[6,3,2,4,2,32,128]{6,5,4,3,2,1,0:T(8,128)S(1)} %get-tuple-element.4.handed, f32[4,8,128]{2,1,0:T(8,128)S(1)} %get-tuple-element.5.scalars), custom_call_target="tpu_custom_call" | custom-call | tf_op jit(solution)/shard_map/pallas_call | solution.py:902

commit v7 on v6

--- a/solution.py
+++ b/solution.py
@@ -755,8 +755,9 @@
             high_magnetic(last)
             high_electric(last)
             form_up(last - 1)
+            send_up(last - 1)
             form_up(last)
-            send_up(last - 1, last)
+            send_up(last)
             wait_up(last - 1)
             low(last - 1)
             send_down(last - 1)

time: 53 us -> 53 us (level)
  no operation moved by 1% of the time
where the time goes in v7:
time: 53 us; the launch traced here: 52.9 us
  Pallas kernels  51.6 us (97%)
  between operations  1.28 us (2%)
    pallas_call x1, Pallas kernels, body(): pl.pallas_call(functools.partial(kernel, nx, ny), out_shape=(jax.ShapeDty...  50 us
    pallas_call x1, Pallas kernels, body(): pl.pallas_call(finish, out_shape=(jax.ShapeDtypeStruct(source.shape, f32)...  1.56 us

profile of v7, /device:TPU:69, one launch (start us, length us, event | category | flops | bytes accessed | tf_op | source)
XLA Modules:
  0.0 52.9 jit_solution(5060676383416997843)
XLA Ops:
  1.3 50.0 %shard_map.50 = (f32[6,3,2,4,2,32,128]{6,5,4,3,2,1,0:T(8,128)S(1)}, f32[4,8,128]{2,1,0:T(8,128)S(1)}) custom-call(f32[1,3,2,4,32,256]{5,4,3,2,1,0:T(8,128)} %source.1, f32[3,4,32,256]{3,2,1,0:T(8,128)} %permittivity.1, f32[1]{0:T(128)S(6)} %copy.5.frequency), custom_call_target="tpu_custom_call" | custom-call | tf_op jit(solution)/shard_map/pallas_call | solution.py:863
  51.3 1.6 %shard_map.51 = (f32[1,3,2,4,32,256]{5,4,3,2,1,0:T(8,128)}, f32[1,3,2,4,32,256]{5,4,3,2,1,0:T(8,128)}) custom-call(f32[6,3,2,4,2,32,128]{6,5,4,3,2,1,0:T(8,128)S(1)} %get-tuple-element.4.handed, f32[4,8,128]{2,1,0:T(8,128)S(1)} %get-tuple-element.5.scalars), custom_call_target="tpu_custom_call" | custom-call | tf_op jit(solution)/shard_map/pallas_call | solution.py:903
